TPU v7x, 128 devices: a whole 4x4x4 slice. The times are simulated.
128 devices in a mesh: dp: 8 (over x, y_hi), expert: 16 (over z, y_lo, core).
Axes of the slice: x: 4, y: 4 (y_hi: 2, y_lo: 2; y = y_hi * 2 + y_lo), z: 4, core: 2. Of those that a mesh axis runs over, the one named last changes fastest.
Arguments:
- tokens: bfloat16 [16384, 4096], P(('dp', 'expert')), may hold values from -6 to 6
- cotangent: bfloat16 [16384, 4096], P(('dp', 'expert')), may hold values from -3 to 3
- expert_ids: int32 [16384, 8, 2], P(('dp', 'expert')), may hold values from 0 to 31, as said below
- slot_ids: int32 [16384, 8, 2], P(('dp', 'expert')), may hold values from 0 to 63, as said below
- route_probs: bfloat16 [16384, 8, 2], P(('dp', 'expert')), may hold values from 0.099609375 to 1
- weights_in: bfloat16 [32, 2, 1792, 512], P('expert', None, 'dp'), may hold values from -0.25 to 0.25
- weights_out: bfloat16 [32, 1792, 512], P('expert', 'dp'), may hold values from -0.125 to 0.125
Outputs:
- grad_tokens: bfloat16 [16384, 4096], P(('dp', 'expert'))
- grad_probs: float32 [16384, 8, 2], P(('dp', 'expert'))
- grad_in: bfloat16 [32, 2, 1792, 512], P('expert', None, 'dp')
- grad_out: bfloat16 [32, 1792, 512], P('expert', 'dp')
Inputs may be any that keep to these rules, and one draw needn't show every extreme that they name: `expert_ids`: each sub-token names 2 different experts. On each device the experts fall into two sets of 16, and the two ids of a sub-token come one from each set. Every expert is named by exactly 64 sub-tokens of every device. `slot_ids`: for each device and expert, the sub-tokens of that device that name the expert carry distinct slot numbers at the matching position.
All inputs are finite; a program needn't handle non-finite values.
Results may differ from a plain program's by a relative error of at most 0.012.
Values may be sent and summed in bfloat16 or wider, within the bound.
A program may use at most 192 MiB of HBM per device.

v0:
```python
import math

import jax
import jax.numpy as jnp
from jax import lax
from jax.sharding import PartitionSpec as P

H = 8
DS = 512


def side_by_side(arrays, axis, split_dim, concat_dim, along):
    widths = [math.prod(a.shape[along:]) for a in arrays]
    both = jnp.concatenate(
        [a.reshape(*a.shape[:along], w) for a, w in zip(arrays, widths)], axis=along
    )
    filled = lax.all_to_all(both, axis, split_axis=split_dim, concat_axis=concat_dim, tiled=True)
    tiles = jnp.split(filled, [sum(widths[:k]) for k in range(1, len(widths))], axis=along)
    return tuple(
        (b.reshape(*filled.shape[:along], *a.shape[along:]) for a, b in zip(arrays, tiles))
    )


def rows_first(arrays, axis, dims):
    turned = [jnp.moveaxis(a, dim, 0) for a, dim in zip(arrays, dims)]
    widths = [t[0].size for t in turned]
    both = jnp.concatenate([t.reshape(-1, w) for t, w in zip(turned, widths)], axis=1)
    filled = lax.all_gather(both, axis, axis=0, tiled=True)
    tiles = jnp.split(filled, [sum(widths[:k]) for k in range(1, len(widths))], axis=1)
    return tuple(
        (
            jnp.moveaxis(b.reshape(-1, *t.shape[1:]), 0, dim)
            for b, t, dim in zip(tiles, turned, dims)
        )
    )


def contract_last(former, latter):
    return lax.dot_general(
        former, latter, (((1,), (1,)), ((), ())), preferred_element_type=jnp.float32
    )


def expert_backward(inputs, cotangent, weighting, gate_up, down_proj):
    gate_pre = contract_last(inputs, gate_up[0])
    up_pre = contract_last(inputs, gate_up[1])
    sigmoids = jax.nn.sigmoid(gate_pre)
    activated = gate_pre * sigmoids
    hidden = (activated * up_pre).astype(jnp.bfloat16)
    output = jnp.dot(hidden, down_proj, preferred_element_type=jnp.float32)
    router_grad = jnp.sum(output * cotangent.astype(jnp.float32), axis=1).astype(jnp.bfloat16)
    scaled = (weighting.astype(jnp.float32)[:, None] * cotangent.astype(jnp.float32)).astype(
        jnp.bfloat16
    )
    dhidden = contract_last(scaled, down_proj)
    gate_grad = (dhidden * up_pre * sigmoids * (1.0 + gate_pre * (1.0 - sigmoids))).astype(
        jnp.bfloat16
    )
    up_grad = (dhidden * activated).astype(jnp.bfloat16)
    input_grad = jnp.dot(gate_grad, gate_up[0], preferred_element_type=jnp.float32)
    input_grad = (
        input_grad + jnp.dot(up_grad, gate_up[1], preferred_element_type=jnp.float32)
    ).astype(jnp.bfloat16)
    return (input_grad, router_grad, gate_grad, up_grad, hidden, scaled)


def reduce_grads(inputs, gate_grad, up_grad, hidden, scaled):
    gate_term = jnp.einsum("rf,rd->fd", gate_grad, inputs, preferred_element_type=jnp.float32)
    up_term = jnp.einsum("rf,rd->fd", up_grad, inputs, preferred_element_type=jnp.float32)
    summed = lax.psum_scatter(
        jnp.concatenate(
            [
                jnp.stack([gate_term, up_term], axis=1),
                jnp.einsum("rf,rd->fd", hidden, scaled, preferred_element_type=jnp.float32)[
                    :, None, :
                ],
            ],
            axis=1,
        ).astype(jnp.bfloat16),
        "dp",
        scatter_dimension=0,
        tiled=True,
    ).astype(jnp.float32)
    pair_sum = summed[:, :2]
    down_sum = summed[:, 2]
    return (jnp.transpose(pair_sum, (1, 0, 2)).astype(jnp.bfloat16), down_sum.astype(jnp.bfloat16))


def body(tokens, cotangent, expert_ids, slot_ids, route_probs, weights_in, weights_out):
    peers = lax.axis_size("expert")
    local_count = weights_in.shape[0]
    token_count = tokens.shape[0]
    sub_count = token_count * H
    capacity = sub_count * 2 // (local_count * peers)
    buffer_rows = local_count * peers * capacity
    chosen = expert_ids.reshape(sub_count, 2)
    placed = (
        chosen % local_count * (peers * capacity)
        + chosen // local_count * capacity
        + slot_ids.reshape(sub_count, 2)
    )
    flat_place = placed.reshape(-1)

    def spread(values):
        doubled = jnp.broadcast_to(values[:, None, :], (sub_count, 2, DS)).reshape(
            2 * sub_count, DS
        )
        filled = jnp.zeros((buffer_rows, DS), jnp.bfloat16).at[flat_place].set(doubled)
        return filled.reshape(local_count, peers, capacity, DS)

    input_buffer = spread(tokens.reshape(sub_count, DS))
    cotangent_buffer = spread(cotangent.reshape(sub_count, DS))
    prob_buffer = (
        jnp.zeros((buffer_rows,), jnp.bfloat16).at[flat_place].set(route_probs.reshape(-1))
    )
    prob_buffer = prob_buffer.reshape(local_count, peers, capacity)
    arrived_in = lax.all_to_all(input_buffer, "expert", split_axis=1, concat_axis=1, tiled=True)
    arrived_cot, arrived_prob = side_by_side((cotangent_buffer, prob_buffer), "expert", 1, 1, 3)
    input_grads = []
    router_grads = []
    grads_pair = []
    grads_down = []
    for expert_pos in range(local_count):
        single_in, single_out = rows_first(
            (weights_in[expert_pos : expert_pos + 1], weights_out[expert_pos : expert_pos + 1]),
            "dp",
            (2, 1),
        )
        gate_up = single_in[0]
        down_proj = single_out[0]
        rows_in = arrived_in[expert_pos].reshape(peers * capacity, DS)
        rows_cot = arrived_cot[expert_pos].reshape(peers * capacity, DS)
        rows_prob = arrived_prob[expert_pos].reshape(peers * capacity)
        input_grad, router_grad, gate_grad, up_grad, hidden, scaled = expert_backward(
            rows_in, rows_cot, rows_prob, gate_up, down_proj
        )
        pair_part, down_part = reduce_grads(rows_in, gate_grad, up_grad, hidden, scaled)
        input_grads.append(input_grad)
        router_grads.append(router_grad)
        grads_pair.append(pair_part)
        grads_down.append(down_part)
    stacked_inputs = jnp.stack(input_grads).reshape(local_count, peers, capacity, DS)
    stacked_router = jnp.stack(router_grads).reshape(local_count, peers, capacity)
    returned, returned_router = side_by_side((stacked_inputs, stacked_router), "expert", 1, 1, 3)
    back_rows = (
        returned.reshape(buffer_rows, DS)[flat_place].reshape(sub_count, 2, DS).astype(jnp.float32)
    )
    grad_tokens = jnp.sum(back_rows, axis=1).astype(jnp.bfloat16).reshape(token_count, H * DS)
    grad_probs = (
        returned_router.reshape(buffer_rows)[flat_place]
        .reshape(token_count, H, 2)
        .astype(jnp.float32)
    )
    return (grad_tokens, grad_probs, jnp.stack(grads_pair), jnp.stack(grads_down))


def solution(mesh):
    return jax.shard_map(
        body,
        mesh=mesh,
        in_specs=(
            P(("dp", "expert"), None),
            P(("dp", "expert"), None),
            P(("dp", "expert"), None, None),
            P(("dp", "expert"), None, None),
            P(("dp", "expert"), None, None),
            P("expert", None, "dp", None),
            P("expert", "dp", None),
        ),
        out_specs=(
            P(("dp", "expert"), None),
            P(("dp", "expert"), None, None),
            P("expert", None, "dp", None),
            P("expert", "dp", None),
        ),
        check_vma=False,
    )
```

profile of v0, /device:TPU:0, one launch (start us, length us, event | category | flops | bytes accessed | tf_op | source)
XLA Modules:
  0.0 402.9 jit_solution(530225747279303801)
XLA Ops:
  17.7 10.6 %scatter_custom_fusion.2 = bf16[2048,512]{1,0:T(8,128)(2,1)S(1)} fusion(s32[2048]{0:T(1024)S(1)} %bitcast.149, bf16[2048,512]{1,0:T(8,128)(2,1)} %reshape.320, bf16[]{:T(256)} %constant.31.clone.1), kind=kCustom, calls=%fused_computation.59 | custom fusion | bytes 2097664 | tf_op jit(solution)/shard_map/scatter | solution.py:108
  29.8 6.8 %all-to-all-start.1 = ((bf16[2,16,64,512]{3,2,0,1:T(8,128)(2,1)}), bf16[2,16,64,512]{3,2,0,1:T(8,128)(2,1)S(1)}, u32[]{:S(2)}, u32[]{:S(2)}) async-start(bf16[2,16,64,512]{3,2,0,1:T(8,128)(2,1)} %copy.47), calls=%async_computation.1 | async-start | bytes 4194304 | tf_op jit(solution)/shard_map/all_to_all | solution.py:117
  37.1 14.6 %scatter_custom_fusion.1 = bf16[2048]{0:T(1024)(128)(2,1)S(1)} fusion(s32[2048]{0:T(1024)S(1)} %bitcast.150, bf16[2048]{0:T(1024)(128)(2,1)S(1)} %reshape.312, bf16[]{:T(256)} %constant.31.clone.1), kind=kCustom, calls=%fused_computation.88 | custom fusion | bytes 4098 | tf_op jit(solution)/shard_map/scatter | solution.py:114
  61.7 11.5 %scatter_custom_fusion = bf16[2048,512]{1,0:T(8,128)(2,1)} fusion(s32[2048]{0:T(1024)S(1)} %bitcast.151, bf16[2048,512]{1,0:T(8,128)(2,1)} %reshape.304, bf16[]{:T(256)} %constant.31.clone.1), kind=kCustom, calls=%fused_computation.61 | custom fusion | bytes 2097664 | tf_op jit(solution)/shard_map/scatter | solution.py:108
  78.3 5.8 %all-to-all-start = ((bf16[2,16,64,513]{3,2,0,1:T(8,128)(2,1)}), bf16[2,16,64,513]{3,2,0,1:T(8,128)(2,1)S(1)}, u32[]{:S(2)}, u32[]{:S(2)}) async-start(bf16[2,16,64,513]{3,2,0,1:T(8,128)(2,1)} %copy.44), calls=%async_computation | async-start | bytes 5242880 | tf_op jit(solution)/shard_map/all_to_all | solution.py:17
  87.3 35.7 %all-to-all-done = bf16[2,16,64,513]{3,2,0,1:T(8,128)(2,1)S(1)} async-done(((bf16[2,16,64,513]{3,2,0,1:T(8,128)(2,1)}), bf16[2,16,64,513]{3,2,0,1:T(8,128)(2,1)S(1)}, u32[]{:S(2)}, u32[]{:S(2)}) %all-to-all-start) | async-done | bytes 2101280 | tf_op jit(solution)/shard_map/all_to_all | solution.py:17
  130.1 7.6 %reshape.275 = bf16[1792,1,2,512]{3,2,0,1:T(2,128)(2,1)} reshape(bf16[1792,1024]{1,0:T(8,128)(2,1)} %split.29) | data formatting | bytes 7340032 | tf_op jit(solution)/shard_map/reshape | solution.py:32
  142.6 6.6 %fusion.17 = f32[1024,1792]{1,0:T(8,128)} fusion(bf16[1024,512]{1,0:T(8,128)(2,1)S(1)} %multiply_convert_fusion.6, bf16[1792,1536]{1,0:T(8,128)(2,1)} %all-gather.5.cloned.1.call-done), kind=kOutput, calls=%fused_computation.52 | convolution fusion | flops 1879048192 | bytes 10223616 | tf_op jit(solution)/shard_map/dot_general | solution.py:39
  149.3 9.4 %multiply_convert_fusion.3 = (bf16[1024,1792]{1,0:T(8,128)(2,1)S(1)}, bf16[1024,1792]{1,0:T(8,128)(2,1)}, bf16[1024,1792]{1,0:T(8,128)(2,1)}) fusion(f32[1024,1792]{1,0:T(8,128)} %fusion.17, f32[1024,1792]{1,0:T(8,128)S(1)} %fusion.13, bf16[1024,512]{1,0:T(8,128)(2,1)S(1)} %bitcast.146, bf16[1,2,1792,512]{3,2,1,0:T(8,128)(2,1)S(1)} %bitcast.128), kind=kOutput, calls=%fused_computation.8 | convolution fusion | flops 1906573312 | bytes 28573696 | tf_op jit(solution)/shard_map/dot_general | solution.py:39
  158.7 5.5 %fusion.7 = bf16[1792,1,512]{2,0,1:T(8,128)(2,1)S(1)} fusion(bf16[1024,1792]{1,0:T(8,128)(2,1)} %get-tuple-element.22, bf16[1024,512]{1,0:T(8,128)(2,1)S(1)} %multiply_convert_fusion.6), kind=kOutput, calls=%fused_computation.30 | convolution fusion | flops 1879965696 | bytes 6553600 | tf_op jit(solution)/shard_map/rf,rd->fd/dot_general | solution.py:74
  173.1 21.6 %all-gather.3.cloned.1.call-done = bf16[1792,1536]{1,0:T(8,128)(2,1)} async-done(((bf16[224,1536]{1,0:T(8,128)(2,1)}), bf16[1792,1536]{1,0:T(8,128)(2,1)}) %all-gather.3.cloned.1.call-update) | async-done | bytes 5505040 | tf_op jit(solution)/shard_map/all_gather | solution.py:28
  198.9 7.3 %reshape.273 = bf16[1792,1,2,512]{3,2,0,1:T(2,128)(2,1)} reshape(bf16[1792,1024]{1,0:T(8,128)(2,1)} %split.27) | data formatting | bytes 7340032 | tf_op jit(solution)/shard_map/reshape | solution.py:32
  211.0 6.5 %fusion.20 = f32[1024,1792]{1,0:T(8,128)} fusion(bf16[1024,512]{1,0:T(8,128)(2,1)S(1)} %multiply_convert_fusion.7, bf16[1792,1536]{1,0:T(8,128)(2,1)} %all-gather.3.cloned.1.call-done), kind=kOutput, calls=%fused_computation.55 | convolution fusion | flops 1879048192 | bytes 10223616 | tf_op jit(solution)/shard_map/dot_general | solution.py:39
  217.6 9.6 %multiply_convert_fusion.5 = (bf16[1024,1792]{1,0:T(8,128)(2,1)S(1)}, bf16[1024,1792]{1,0:T(8,128)(2,1)}, bf16[1024,1792]{1,0:T(8,128)(2,1)}) fusion(f32[1024,1792]{1,0:T(8,128)} %fusion.20, f32[1024,1792]{1,0:T(8,128)S(1)} %fusion.9, bf16[1024,512]{1,0:T(8,128)(2,1)S(1)} %bitcast.142, bf16[1,2,1792,512]{3,2,1,0:T(8,128)(2,1)S(1)} %bitcast.132), kind=kOutput, calls=%fused_computation.12 | convolution fusion | flops 1906573312 | bytes 28573696 | tf_op jit(solution)/shard_map/dot_general | solution.py:39
  227.2 5.5 %fusion.4 = bf16[1792,1,512]{2,0,1:T(8,128)(2,1)S(1)} fusion(bf16[1024,1792]{1,0:T(8,128)(2,1)} %get-tuple-element.19, bf16[1024,512]{1,0:T(8,128)(2,1)S(1)} %multiply_convert_fusion.7), kind=kOutput, calls=%fused_computation.27 | convolution fusion | flops 1879965696 | bytes 6553600 | tf_op jit(solution)/shard_map/rf,rd->fd/dot_general | solution.py:74
  248.2 5.7 %multiply_reduce_fusion = bf16[1024]{0:T(1024)(128)(2,1)S(1)} fusion(f32[1024,512]{0,1:T(8,128)} %copy.55, bf16[1024,1792]{1,0:T(8,128)(2,1)} %get-tuple-element.22, bf16[1792,1536]{1,0:T(8,128)(2,1)} %all-gather.5.cloned.1.call-done), kind=kOutput, calls=%fused_computation.33 | convolution fusion | flops 1880095744 | bytes 7604224 | tf_op jit(solution)/shard_map/dot_general | solution.py:50
  253.9 4.7 %multiply_reduce_fusion.1 = bf16[1024]{0:T(1024)(128)(2,1)S(1)} fusion(f32[1024,512]{0,1:T(8,128)S(1)} %copy-done.10, bf16[1024,1792]{1,0:T(8,128)(2,1)} %get-tuple-element.19, bf16[1792,1536]{1,0:T(8,128)(2,1)} %all-gather.3.cloned.1.call-done), kind=kOutput, calls=%fused_computation.34 | convolution fusion | flops 1880095744 | bytes 7604224 | tf_op jit(solution)/shard_map/dot_general | solution.py:50
  259.1 4.8 %fusion.12 = f32[1024,512]{1,0:T(8,128)S(1)} fusion(bf16[1024,1792]{1,0:T(8,128)(2,1)} %get-tuple-element.23, bf16[1,2,1792,512]{3,2,1,0:T(8,128)(2,1)} %bitcast.129), kind=kOutput, calls=%fused_computation.47 | convolution fusion | flops 1879048192 | bytes 7602176 | tf_op jit(solution)/shard_map/dot_general | solution.py:62
  273.1 5.2 %all-to-all-start.2 = ((bf16[2,16,64,513]{3,2,0,1:T(8,128)(2,1)}), bf16[2,16,64,513]{3,2,0,1:T(8,128)(2,1)S(1)}, u32[]{:S(2)}, u32[]{:S(2)}) async-start(bf16[2,16,64,513]{3,2,0,1:T(8,128)(2,1)} %pad_maximum_fusion.3), calls=%async_computation.2 | async-start | bytes 5242880 | tf_op jit(solution)/shard_map/all_to_all | solution.py:17
  278.3 39.6 %all-to-all-done.2 = bf16[2,16,64,513]{3,2,0,1:T(8,128)(2,1)S(1)} async-done(((bf16[2,16,64,513]{3,2,0,1:T(8,128)(2,1)}), bf16[2,16,64,513]{3,2,0,1:T(8,128)(2,1)S(1)}, u32[]{:S(2)}, u32[]{:S(2)}) %all-to-all-start.2) | async-done | bytes 2101280 | tf_op jit(solution)/shard_map/all_to_all | solution.py:17
  319.8 9.2 %gather_fusion = bf16[2048,512]{1,0:T(8,128)(2,1)} fusion(bf16[2048,512]{1,0:T(8,128)(2,1)S(1)} %bitcast.124, s32[2048]{0:T(1024)S(1)} %broadcast_clamp_fusion), kind=kCustom, calls=%fused_computation | custom fusion | bytes 4202496 | tf_op jit(solution)/shard_map/gather | solution.py:146
  331.8 6.7 %reduce_sum.32 = bf16[1024,512]{1,0:T(8,128)(2,1)} reduce(bf16[1024,2,512]{2,1,0:T(2,128)(2,1)S(1)} %reshape.277, bf16[]{:T(256)} %constant.31.clone.1), dimensions={1}, to_apply=%region_5.6 | reduce | flops 524288 | bytes 3145730 | tf_op jit(solution)/shard_map/reduce_sum | solution.py:148
  341.2 13.1 %gather_fusion.1 = bf16[2048]{0:T(1024)(128)(2,1)S(1)} fusion(bf16[2048]{0:T(1024)(128)(2,1)S(1)} %reshape_reshape.8, s32[2048]{0:T(1024)S(1)} %broadcast_clamp_fusion), kind=kCustom, calls=%fused_computation.1 | custom fusion | bytes 16384 | tf_op jit(solution)/shard_map/gather | solution.py:150
  356.6 34.6 %reduce-scatter.3.cloned.1.call-done = bf16[224,3,512]{2,0,1:T(8,128)(2,1)} async-done(((bf16[1792,3,512]{2,0,1:T(8,128)(2,1)}), bf16[224,3,512]{2,0,1:T(8,128)(2,1)}) %reduce-scatter.3.cloned.1.call-update) | async-done | bytes 688144 | tf_op jit(solution)/shard_map/reduce_scatter | solution.py:70
  (132 shorter events, 100.0 us)
Async XLA Ops:
  7.2 118.8 %all-gather.5.cloned.1.call-start = ((), (), s32[]{:S(2)}) async-start(), calls=%async_computation.6 | async-start | bytes 6193152 | tf_op jit(solution)/shard_map/all_gather | solution.py:28
  10.1 3.0 copy-start.15
  11.0 2.8 copy-start.11
  11.0 183.6 %all-gather.3.cloned.1.call-start = ((), (), s32[]{:S(2)}) async-start(), calls=%async_computation.5 | async-start | bytes 6193152 | tf_op jit(solution)/shard_map/all_gather | solution.py:28
  28.3 8.3 %copy-start.16 = (bf16[128,8,2]{0,2,1:T(2,128)(2,1)S(1)}, bf16[128,8,2]{0,2,1:T(2,128)(2,1)}, u32[]{:S(2)}) copy-start(bf16[128,8,2]{0,2,1:T(2,128)(2,1)} %param.11) | copy-start | bytes 12292
  29.8 47.2 %all-to-all-start.1 = ((bf16[2,16,64,512]{3,2,0,1:T(8,128)(2,1)}), bf16[2,16,64,512]{3,2,0,1:T(8,128)(2,1)S(1)}, u32[]{:S(2)}, u32[]{:S(2)}) async-start(bf16[2,16,64,512]{3,2,0,1:T(8,128)(2,1)} %copy.47), calls=%async_computation.1 | async-start | bytes 4194304 | tf_op jit(solution)/shard_map/all_to_all | solution.py:117
  57.5 15.7 %copy-start.9 = (bf16[2,16,64,1]{3,2,1,0:T(8,128)(2,1)S(1)}, bf16[2,16,64,1]{3,2,1,0:T(8,128)(2,1)}, u32[]{:S(2)}) copy-start(bf16[2,16,64,1]{3,2,1,0:T(8,128)(2,1)} %reshape_reshape.9) | copy-start | bytes 12292
  78.3 44.7 %all-to-all-start = ((bf16[2,16,64,513]{3,2,0,1:T(8,128)(2,1)}), bf16[2,16,64,513]{3,2,0,1:T(8,128)(2,1)S(1)}, u32[]{:S(2)}, u32[]{:S(2)}) async-start(bf16[2,16,64,513]{3,2,0,1:T(8,128)(2,1)} %copy.44), calls=%async_computation | async-start | bytes 5242880 | tf_op jit(solution)/shard_map/all_to_all | solution.py:17
  84.1 271.5 %reduce-scatter.5.cloned.1.call-start = ((), (), s32[]{:S(2)}) async-start(), calls=%async_computation.8 | async-start | bytes 6193152 | tf_op jit(solution)/shard_map/reduce_scatter | solution.py:70
  137.8 2.8 copy-start.13
  140.5 8.8 %copy-start.5 = (bf16[1792,1,2,512]{3,0,2,1:T(8,128)(2,1)}, bf16[1792,1,2,512]{3,0,2,1:T(8,128)(2,1)S(1)}, u32[]{:S(2)}) copy-start(bf16[1792,1,2,512]{3,0,2,1:T(8,128)(2,1)S(1)} %copy.66) | copy-start | bytes 11010052
  158.7 7.7 %copy-start.17 = (bf16[1024,1792]{1,0:T(8,128)(2,1)}, bf16[1024,1792]{1,0:T(8,128)(2,1)S(1)}, u32[]{:S(2)}) copy-start(bf16[1024,1792]{1,0:T(8,128)(2,1)S(1)} %get-tuple-element.21) | copy-start | bytes 11010052
  158.7 5.5 %copy-start.21 = (bf16[1024,1792]{1,0:T(8,128)(2,1)S(1)}, bf16[1024,1792]{1,0:T(8,128)(2,1)}, u32[]{:S(2)}) copy-start(bf16[1024,1792]{1,0:T(8,128)(2,1)} %get-tuple-element.23) | copy-start | bytes 11010052
  171.6 219.6 %reduce-scatter.3.cloned.1.call-start = ((), (), s32[]{:S(2)}) async-start(), calls=%async_computation.7 | async-start | bytes 6193152 | tf_op jit(solution)/shard_map/reduce_scatter | solution.py:70
  206.2 2.7 copy-start.12
  208.9 8.7 %copy-start.7 = (bf16[1792,1,2,512]{3,0,2,1:T(8,128)(2,1)}, bf16[1792,1,2,512]{3,0,2,1:T(8,128)(2,1)S(1)}, u32[]{:S(2)}) copy-start(bf16[1792,1,2,512]{3,0,2,1:T(8,128)(2,1)S(1)} %copy.67) | copy-start | bytes 11010052
  227.2 7.7 %copy-start.19 = (bf16[1024,1792]{1,0:T(8,128)(2,1)}, bf16[1024,1792]{1,0:T(8,128)(2,1)S(1)}, u32[]{:S(2)}) copy-start(bf16[1024,1792]{1,0:T(8,128)(2,1)S(1)} %get-tuple-element.18) | copy-start | bytes 11010052
  227.2 5.5 %copy-start.22 = (bf16[1024,1792]{1,0:T(8,128)(2,1)S(1)}, bf16[1024,1792]{1,0:T(8,128)(2,1)}, u32[]{:S(2)}) copy-start(bf16[1024,1792]{1,0:T(8,128)(2,1)} %get-tuple-element.20) | copy-start | bytes 11010052
  248.2 5.7 %copy-start.10 = (f32[1024,512]{0,1:T(8,128)S(1)}, f32[1024,512]{0,1:T(8,128)}, u32[]{:S(2)}) copy-start(f32[1024,512]{0,1:T(8,128)} %copy.54) | copy-start | bytes 6291460
  259.1 4.8 %copy-start.8 = (bf16[1792,1,2,512]{3,0,2,1:T(8,128)(2,1)S(1)}, bf16[1792,1,2,512]{3,0,2,1:T(8,128)(2,1)}, u32[]{:S(2)}) copy-start(bf16[1792,1,2,512]{3,0,2,1:T(8,128)(2,1)} %copy-done.7) | copy-start | bytes 11010052
  259.1 4.8 %copy-start.23 = (bf16[1024,1792]{1,0:T(8,128)(2,1)S(1)}, bf16[1024,1792]{1,0:T(8,128)(2,1)}, u32[]{:S(2)}) copy-start(bf16[1024,1792]{1,0:T(8,128)(2,1)} %get-tuple-element.20) | copy-start | bytes 11010052
  264.0 3.2 copy-start.18
  273.1 44.8 %all-to-all-start.2 = ((bf16[2,16,64,513]{3,2,0,1:T(8,128)(2,1)}), bf16[2,16,64,513]{3,2,0,1:T(8,128)(2,1)S(1)}, u32[]{:S(2)}, u32[]{:S(2)}) async-start(bf16[2,16,64,513]{3,2,0,1:T(8,128)(2,1)} %pad_maximum_fusion.3), calls=%async_computation.2 | async-start | bytes 5242880 | tf_op jit(solution)/shard_map/all_to_all | solution.py:17
  331.8 9.0 %slice-start = ((bf16[2,16,64,513]{3,2,0,1:T(8,128)(2,1)}), bf16[2,16,64,1]{3,2,0,1:T(8,128)(2,1)S(1)}, s32[]{:S(2)}) async-start(bf16[2,16,64,513]{3,2,0,1:T(8,128)(2,1)} %copy-done), calls=%async_computation.9 | async-start | bytes 1048576 | tf_op jit(solution)/shard_map/split | solution.py:18
  (8 other events, 13.1 us)
Sparse Core Ops, SparseCore 0:
  11.1 101.8 all-gather.4
  115.4 79.2 all-gather.2
  198.6 91.2 reduce-scatter.4
  293.7 97.4 reduce-scatter.2
where the time goes:
time: 410 us; the launch traced here: 403 us
  local copies, waits for them, and re-layouts  138 us (34%)
  waiting for transfers between devices  132 us (32%)
  matrix products  77.4 us (19%)
  other arithmetic  23.1 us (6%)
  starting transfers between devices  17.9 us (4%)
  between operations  14.7 us (4%)
    all_to_all x2, waiting for transfers between devices, side_by_side(): lax.all_to_all(both, axis, split_axis=split_dim, concat_axis=concat_dim,...  75.3 us
    dot_general x6, matrix products, contract_last(): lax.dot_general(former, latter, (((1,), (1,)), ((), ())), preferred_eleme...  36.4 us
    reduce_scatter x2, waiting for transfers between devices, reduce_grads(): lax.psum_scatter(jnp.concatenate([jnp.stack([gate_term, up_term], axis=1)...  34.6 us
    scatter x2, local copies, waits for them, and re-layouts, spread(): jnp.zeros((buffer_rows, DS), jnp.bfloat16).at[flat_place].set(doubled)  22.1 us
    all_gather x2, waiting for transfers between devices, rows_first(): filled = lax.all_gather(both, axis, axis=0, tiled=True)  21.6 us
    reshape x4, local copies, waits for them, and re-layouts, rows_first(): b.reshape(-1, *t.shape[1:])  20.4 us
    scatter x1, local copies, waits for them, and re-layouts, body(): jnp.zeros((buffer_rows,), jnp.bfloat16).at[flat_place]  14.6 us
    gather x1, local copies, waits for them, and re-layouts, body(): returned_router.reshape(buffer_rows)[flat_place].reshape(token_count, H, 2)  13.1 us
  transfers between devices with their start and end apart: 7, of which 4 were waited for; matrix products, arithmetic and copies ran while one was open for 55% of the time, Pallas kernels for 0%

commit v1 on v0

v1 whole, which is shorter than its diff:
```python
import functools

import jax
import jax.numpy as jnp
from jax import lax
from jax.experimental import pallas as pl
from jax.experimental.pallas import tpu as pltpu
from jax.sharding import PartitionSpec as P

H = 8
NX = 4
NH = 2
MESH = pl.DeviceIdType.MESH
F32 = jnp.float32
BF16 = jnp.bfloat16
GROUP = 4
JB = 256


def dot_nn(a, b):
    return lax.dot_general(a, b, (((1,), (0,)), ((), ())), preferred_element_type=F32)


def dot_nt(a, b):
    return lax.dot_general(a, b, (((1,), (1,)), ((), ())), preferred_element_type=F32)


def dot_tn(a, b):
    return lax.dot_general(a, b, (((0,), (0,)), ((), ())), preferred_element_type=F32)


def kernel(
    dims,
    tok,
    cot,
    place_row,
    prob_row,
    place_col,
    w_in,
    w_out,
    gtok,
    gprob,
    gin,
    gout,
    tok_rows,
    cot_rows,
    x_send,
    s_send,
    x_all,
    s_all,
    wall,
    acts,
    dxt,
    racc,
    part,
    rs_far,
    rs_sum,
    rs_dir,
    stage,
    swap,
    dx_send,
    back,
    r_send,
    r_back,
    gacc,
    w_ssem,
    w_rsem,
    x_ssem,
    x_rsem,
    s_ssem,
    s_rsem,
    g_ssem,
    g_rsem,
    d_ssem,
    d_rsem,
    r_ssem,
    r_rsem,
):
    ng, toks, d, fs, cap = dims
    experts = NH * ng
    peers = NH * ng
    rows = toks * H
    slots = peers * cap
    half = fs // 2
    fc = NH * fs

    dp = lax.axis_index("dp")
    g = lax.axis_index("expert")
    x = dp // NH
    h = dp % NH
    right = (x + 1) % NX
    left = (x + 3) % NX
    far = (x + 2) % NX
    other = 1 - h
    my_e = g * NH + h
    my_b = h * ng + g

    def remote(src, dst, ssem, rsem, to_dp, to_g):
        return pltpu.make_async_remote_copy(
            src_ref=src,
            dst_ref=dst,
            send_sem=ssem,
            recv_sem=rsem,
            device_id=(to_dp, to_g),
            device_id_type=MESH,
        )

    barrier = pltpu.get_barrier_semaphore()

    def greet(t, carry):
        u = (my_b + t) % peers
        pl.semaphore_signal(
            barrier, inc=1, device_id=(x * NH + u // ng, u % ng), device_id_type=MESH
        )
        return carry

    lax.fori_loop(1, peers, greet, 0)
    for nx in (right, left):
        pl.semaphore_signal(barrier, inc=1, device_id=(nx * NH + h, g), device_id_type=MESH)
    pl.semaphore_wait(barrier, peers + 1)

    to_right = (right * NH + h, g)
    to_left = (left * NH + h, g)
    to_partner = (x * NH + other, g)

    def wcopy(k, src, dst, to):
        return remote(src, dst, w_ssem.at[k], w_rsem.at[k], *to)

    first = [
        wcopy(0, w_in.at[other], wall.at[x, pl.ds(0, 2), h], to_partner),
        wcopy(1, w_out.at[other], wall.at[x, 2, h], to_partner),
        wcopy(2, w_in.at[h], wall.at[x, pl.ds(0, 2), h], to_right),
        wcopy(3, w_out.at[h], wall.at[x, 2, h], to_right),
        wcopy(4, w_in.at[h], wall.at[x, pl.ds(0, 2), h], to_left),
        wcopy(5, w_out.at[h], wall.at[x, 2, h], to_left),
    ]
    for c in first:
        c.start()

    for n in range(H):
        tok_rows[n * toks : (n + 1) * toks, :] = tok[:, n * d : (n + 1) * d]
        cot_rows[n * toks : (n + 1) * toks, :] = cot[:, n * d : (n + 1) * d]

    groups = experts // GROUP
    span = GROUP * cap

    def send_expert(e):
        to = (x * NH + e % NH, e // NH)

        @pl.when(e != my_e)
        def _():
            remote(x_send.at[e], x_all.at[my_b], x_ssem.at[e], x_rsem.at[my_b], *to).start()
            remote(s_send.at[e], s_all.at[my_b], s_ssem.at[e], s_rsem.at[my_b], *to).start()

    def dispatch(i, carry):
        gb = (my_e // GROUP + i) % groups
        ids = lax.broadcasted_iota(jnp.int32, (span, rows), 0) + gb * span
        hit0 = place_row[0:1, :] == ids
        hit1 = place_row[1:2, :] == ids
        one = jnp.where(hit0 | hit1, 1.0, 0.0).astype(BF16)
        wgt = jnp.where(hit0, prob_row[0:1, :], jnp.where(hit1, prob_row[1:2, :], 0.0)).astype(BF16)
        x_send[pl.ds(gb * GROUP, GROUP)] = (
            dot_nn(one, tok_rows[...]).astype(BF16).reshape(GROUP, cap, d)
        )
        s_send[pl.ds(gb * GROUP, GROUP)] = (
            dot_nn(wgt, cot_rows[...]).astype(BF16).reshape(GROUP, cap, d)
        )
        for j in range(GROUP):
            send_expert(gb * GROUP + j)
        return carry

    lax.fori_loop(0, groups, dispatch, 0)
    wall[x, 0:2, h] = w_in[h]
    wall[x, 2, h] = w_out[h]
    x_all[my_b] = x_send[my_e]
    s_all[my_b] = s_send[my_e]

    def wforward(k, slot, part_rows, plane, to):
        ref = wall.at[slot, pl.ds(0, 3), plane, part_rows]
        return wcopy(k, ref, ref, to)

    top, bottom, full = pl.ds(0, half), pl.ds(half, half), pl.ds(0, fs)
    first[2].wait_recv()
    first[3].wait_recv()
    f6 = wforward(6, left, top, h, to_right)
    f6.start()
    first[4].wait_recv()
    first[5].wait_recv()
    f7 = wforward(7, right, bottom, h, to_left)
    f7.start()
    first[0].wait_recv()
    first[1].wait_recv()
    f8 = wforward(8, x, full, other, to_right)
    f8.start()
    f9 = wforward(9, x, full, other, to_left)
    f9.start()
    f8.wait_recv()
    f10 = wforward(10, left, top, other, to_right)
    f10.start()
    f9.wait_recv()
    f11 = wforward(11, right, bottom, other, to_left)
    f11.start()

    def arrived(t, carry):
        b = (my_b + t) % peers
        remote(x_send.at[0], x_all.at[b], x_ssem.at[0], x_rsem.at[b], x * NH, g).wait_recv()
        remote(s_send.at[0], s_all.at[b], s_ssem.at[0], s_rsem.at[b], x * NH, g).wait_recv()
        return carry

    lax.fori_loop(1, peers, arrived, 0)
    for c in (f6, f7, f10, f11):
        c.wait_recv()

    racc[...] = jnp.zeros_like(racc)
    dxt[...] = jnp.zeros_like(dxt)

    def chunk(s, carry):
        off = jnp.where(s == 0, 2, jnp.where(s == 1, 1, jnp.where(s == 2, 3, 0)))
        xc = (x + off) % NX

        def block(j, c2):
            at = pl.ds(pl.multiple_of(j * JB, JB), JB)
            some = pl.ds(j * (JB // cap), JB // cap)
            xb = x_all[some].reshape(JB, d)
            sb = s_all[some].reshape(JB, d)
            wg = wall[xc, 0].reshape(fc, d)
            wu = wall[xc, 1].reshape(fc, d)
            wo = wall[xc, 2].reshape(fc, d)
            gate = dot_nt(wg, xb)
            up = dot_nt(wu, xb)
            dh = dot_nt(wo, sb)
            sg = 0.5 * jnp.tanh(0.5 * gate) + 0.5
            a = gate * sg
            du = dh * a
            dg = dh * up * (sg + a * (1.0 - sg))
            hid = a * up
            dgb = dg.astype(BF16)
            dub = du.astype(BF16)
            acts[0, :, at] = dgb
            acts[1, :, at] = dub
            acts[2, :, at] = hid.astype(BF16)
            racc[:, at] += jnp.sum((du * up).reshape(fc // 8, 8, JB), axis=0)
            dxt[:, at] += dot_tn(wg, dgb) + dot_tn(wu, dub)
            return c2

        lax.fori_loop(0, slots // JB, block, 0)
        xa = x_all[...].reshape(slots, d)
        sa = s_all[...].reshape(slots, d)
        part[s, 0] = dot_nn(acts[0], xa).astype(BF16).reshape(NH, fs, d)
        part[s, 1] = dot_nn(acts[1], xa).astype(BF16).reshape(NH, fs, d)
        part[s, 2] = dot_nn(acts[2], sa).astype(BF16).reshape(NH, fs, d)

        @pl.when(s == 0)
        def _():
            far_right.start()
            far_left.start()

        @pl.when(s == 1)
        def _():
            dir_right.start()

        @pl.when(s == 2)
        def _():
            dir_left.start()
            far_right.wait_recv()
            add_far(0, 1, top)
            sum_right.start()
            far_left.wait_recv()
            add_far(1, 2, bottom)
            sum_left.start()

        return carry

    def gcopy(k, src, dst, to):
        return remote(src, dst, g_ssem.at[k], g_rsem.at[k], *to)

    def piece(s, part_rows):
        return part.at[s, pl.ds(0, 3), pl.ds(0, NH), part_rows]

    far_right = gcopy(0, piece(0, top), rs_far.at[0], to_right)
    far_left = gcopy(1, piece(0, bottom), rs_far.at[1], to_left)
    dir_right = gcopy(2, piece(1, bottom), rs_dir.at[0], to_right)
    dir_left = gcopy(3, piece(2, top), rs_dir.at[1], to_left)
    sum_right = gcopy(4, stage.at[0], rs_sum.at[0], to_right)
    sum_left = gcopy(5, stage.at[1], rs_sum.at[1], to_left)

    def add_far(side, s, part_rows):
        for m in range(3):
            stage[side, m] = (
                rs_far[side, m].astype(F32) + part[s, m, :, part_rows, :].astype(F32)
            ).astype(BF16)

    lax.fori_loop(0, NX, chunk, 0)

    def turn(i, carry):
        at = pl.ds(pl.multiple_of(i * 256, 256), 256)
        dx_send[pl.ds(i * (256 // cap), 256 // cap)] = (
            jnp.transpose(dxt[:, at], (1, 0)).astype(BF16).reshape(256 // cap, cap, d)
        )
        return carry

    lax.fori_loop(0, slots // 256, turn, 0)
    r_row = jnp.sum(racc[...], axis=0, keepdims=True)
    for i in range(slots // 128):
        r_send[i] = jnp.broadcast_to(r_row[:, i * 128 : (i + 1) * 128], (8, 128))

    def give(t, carry):
        b = (my_b + t) % peers
        to = (x * NH + b // ng, b % ng)
        remote(dx_send.at[b], back.at[my_e], d_ssem.at[b], d_rsem.at[my_e], *to).start()
        remote(
            r_send.at[b * cap // 128], r_back.at[my_e], r_ssem.at[b], r_rsem.at[my_e], *to
        ).start()
        return carry

    lax.fori_loop(1, peers, give, 0)
    back[my_e] = dx_send[my_b]
    r_back[my_e] = r_send[my_b * cap // 128]

    far_from = [(dir_right, sum_right), (dir_left, sum_left)]
    for pair in far_from:
        for c in pair:
            c.wait_recv()

    def total(m, plane, lower):
        mine = part[3, m, plane, pl.ds(half if lower else 0, half), :].astype(F32)
        if lower:
            got = rs_dir[0, m, plane].astype(F32) + rs_sum[1, m, plane].astype(F32)
        else:
            got = rs_dir[1, m, plane].astype(F32) + rs_sum[0, m, plane].astype(F32)
        return (mine + got).astype(BF16)

    for m in range(3):
        swap[m, 0:half] = total(m, other, False)
        swap[m, half:fs] = total(m, other, True)
    swap_in = gcopy(6, swap.at[pl.ds(0, 2)], gin.at[h], to_partner)
    swap_out = gcopy(7, swap.at[2], gout.at[h], to_partner)
    swap_in.start()
    swap_out.start()
    for m in range(2):
        gin[h, m, 0:half] = total(m, h, False)
        gin[h, m, half:fs] = total(m, h, True)
    gout[h, 0:half] = total(2, h, False)
    gout[h, half:fs] = total(2, h, True)

    def gather_back(t, carry):
        b = (my_b + t) % peers
        e = (b % ng) * NH + b // ng
        remote(dx_send.at[0], back.at[e], d_ssem.at[0], d_rsem.at[e], x * NH, g).wait_recv()
        remote(r_send.at[0], r_back.at[e], r_ssem.at[0], r_rsem.at[e], x * NH, g).wait_recv()
        return carry

    lax.fori_loop(1, peers, gather_back, 0)

    def combine(n, carry):
        at = pl.ds(pl.multiple_of(n * toks, toks), toks)
        pc = place_col[at, :]
        ids = lax.broadcasted_iota(jnp.int32, (toks, slots), 1)
        one = jnp.where((pc[:, 0:1] == ids) | (pc[:, 1:2] == ids), 1.0, 0.0).astype(BF16)
        gacc[at, :] = dot_nn(one, back[...].reshape(slots, d))
        return carry

    lax.fori_loop(0, H, combine, 0)
    for n in range(H):
        gtok[:, n * d : (n + 1) * d] = gacc[n * toks : (n + 1) * toks, :].astype(BF16)

    r_mine = r_back[:, 0, :]
    shift = (my_b % (128 // cap)) * cap
    for k in range(2):
        pr = place_row[k : k + 1, :]
        expert = lax.shift_right_logical(pr, cap.bit_length() - 1)
        slot = lax.bitwise_and(pr, cap - 1)
        pick = jnp.where(
            lax.broadcasted_iota(jnp.int32, (experts, rows), 0) == expert, 1.0, 0.0
        )
        table = lax.dot_general(
            r_mine,
            pick,
            (((0,), (0,)), ((), ())),
            precision=lax.Precision.HIGHEST,
            preferred_element_type=F32,
        )
        lanes = lax.broadcasted_iota(jnp.int32, (128, rows), 0)
        value = jnp.sum(jnp.where(lanes == slot + shift, table, 0.0), axis=0, keepdims=True)
        gprob[k : k + 1, :] = value / prob_row[k : k + 1, :]

    for c in first + [f6, f7, f8, f9, f10, f11]:
        c.wait_send()
    for c in (far_right, far_left, dir_right, dir_left, sum_right, sum_left):
        c.wait_send()
    swap_in.wait()
    swap_out.wait()

    def drain(t, carry):
        b = (my_b + t) % peers
        e = (b % ng) * NH + b // ng
        remote(x_send.at[0], x_all.at[0], x_ssem.at[e], x_rsem.at[0], x * NH, g).wait_send()
        remote(s_send.at[0], s_all.at[0], s_ssem.at[e], s_rsem.at[0], x * NH, g).wait_send()
        remote(dx_send.at[0], back.at[0], d_ssem.at[b], d_rsem.at[0], x * NH, g).wait_send()
        remote(r_send.at[0], r_back.at[0], r_ssem.at[b], r_rsem.at[0], x * NH, g).wait_send()
        return carry

    lax.fori_loop(1, peers, drain, 0)


def body(tokens, cotangent, expert_ids, slot_ids, route_probs, weights_in, weights_out):
    ng = lax.axis_size("expert")
    toks = tokens.shape[0]
    d = tokens.shape[1] // H
    fs = weights_in.shape[2]
    experts = NH * ng
    peers = experts
    rows = toks * H
    cap = rows * 2 // experts
    slots = peers * cap
    half = fs // 2
    fc = NH * fs

    place = jnp.transpose(expert_ids * cap + slot_ids, (2, 1, 0)).reshape(2, rows)
    probs = jnp.transpose(route_probs, (2, 1, 0)).reshape(2, rows).astype(F32)
    place_col = jnp.transpose(place, (1, 0))

    vmem = pl.BlockSpec(memory_space=pltpu.VMEM)
    dma = pltpu.SemaphoreType.DMA
    gtok, gprob, gin, gout = pl.pallas_call(
        functools.partial(kernel, (ng, toks, d, fs, cap)),
        out_shape=(
            jax.ShapeDtypeStruct((toks, H * d), BF16),
            jax.ShapeDtypeStruct((2, rows), F32),
            jax.ShapeDtypeStruct((2, 2, fs, d), BF16),
            jax.ShapeDtypeStruct((2, fs, d), BF16),
        ),
        in_specs=[vmem] * 7,
        out_specs=(vmem,) * 4,
        scratch_shapes=[
            pltpu.VMEM((rows, d), BF16),
            pltpu.VMEM((rows, d), BF16),
            pltpu.VMEM((experts, cap, d), BF16),
            pltpu.VMEM((experts, cap, d), BF16),
            pltpu.VMEM((peers, cap, d), BF16),
            pltpu.VMEM((peers, cap, d), BF16),
            pltpu.VMEM((NX, 3, NH, fs, d), BF16),
            pltpu.VMEM((3, fc, slots), BF16),
            pltpu.VMEM((d, slots), F32),
            pltpu.VMEM((8, slots), F32),
            pltpu.VMEM((NX, 3, NH, fs, d), BF16),
            pltpu.VMEM((2, 3, NH, half, d), BF16),
            pltpu.VMEM((2, 3, NH, half, d), BF16),
            pltpu.VMEM((2, 3, NH, half, d), BF16),
            pltpu.VMEM((2, 3, NH, half, d), BF16),
            pltpu.VMEM((3, fs, d), BF16),
            pltpu.VMEM((peers, cap, d), BF16),
            pltpu.VMEM((experts, cap, d), BF16),
            pltpu.VMEM((slots // 128, 8, 128), F32),
            pltpu.VMEM((experts, 8, 128), F32),
            pltpu.VMEM((rows, d), F32),
            dma((12,)),
            dma((12,)),
            dma((experts,)),
            dma((peers,)),
            dma((experts,)),
            dma((peers,)),
            dma((8,)),
            dma((8,)),
            dma((peers,)),
            dma((experts,)),
            dma((peers,)),
            dma((experts,)),
        ],
        compiler_params=pltpu.CompilerParams(
            collective_id=0, has_side_effects=True, vmem_limit_bytes=66_000_000
        ),
        name="moe_backward",
    )(tokens, cotangent, place, probs, place_col, weights_in, weights_out)
    grad_probs = jnp.transpose(gprob.reshape(2, H, toks), (2, 1, 0))
    return gtok, grad_probs, gin, gout


def solution(mesh):
    return jax.shard_map(
        body,
        mesh=mesh,
        in_specs=(
            P(("dp", "expert"), None),
            P(("dp", "expert"), None),
            P(("dp", "expert"), None, None),
            P(("dp", "expert"), None, None),
            P(("dp", "expert"), None, None),
            P("expert", None, "dp", None),
            P("expert", "dp", None),
        ),
        out_specs=(
            P(("dp", "expert"), None),
            P(("dp", "expert"), None, None),
            P("expert", None, "dp", None),
            P("expert", "dp", None),
        ),
        check_vma=False,
    )
```

time: 410 us -> 201 us (0.49)
  the two profiles are of different devices: /device:TPU:0 before, /device:TPU:97 now
where the time goes in v1:
time: 201 us
  Pallas kernels  193 us (96%)
  local copies, waits for them, and re-layouts  6.08 us (3%)
    pallas_call x1, Pallas kernels, body(): pl.pallas_call(functools.partial(kernel, (ng, toks, d, fs, cap)), out_sha...  193 us
    unnamed x14, local copies, waits for them, and re-layouts  5.08 us

profile of v1, /device:TPU:97, one launch (start us, length us, event | category | flops | bytes accessed | tf_op | source)
XLA Modules:
  0.0 200.9 jit_solution(17090177690383816515)
XLA Ops:
  0.6 0.0 copy-start.4
  0.6 0.7 add_bitcast_fusion
  1.4 0.0 copy-done.4
  1.4 0.6 convert_bitcast_fusion.prob_row
  2.0 0.2 copy.11
  2.2 0.0 copy-start
  2.2 0.8 copy.12.place_row
  3.0 0.0 copy-done
  3.0 192.8 %moe_backward.1 = (bf16[128,4096]{1,0:T(8,128)(2,1)}, f32[2,1024]{1,0:T(2,128)}, bf16[2,2,224,512]{3,2,1,0:T(8,128)(2,1)}, bf16[2,224,512]{2,1,0:T(8,128)(2,1)}) custom-call(bf16[128,4096]{1,0:T(8,128)(2,1)} %tok.1, bf16[128,4096]{1,0:T(8,128)(2,1)} %cot.1, s32[2,1024]{1,0:T(2,128)} %copy.12.place_row, f32[2,1024]{1,0:T(2,128)} %convert_bitcast_fusion.prob_row, ...), custom_call_target="tpu_custom_call" | custom-call | tf_op jit(solution)/shard_map/moe_backward/pallas_call | solution.py:425
  195.8 0.0 copy-start.3
  195.8 0.0 copy-start.1
  195.8 2.4 %copy.18 = bf16[128,4096]{1,0:T(8,128)(2,1)} copy(bf16[128,4096]{1,0:T(8,128)(2,1)} %get-tuple-element.16) | data formatting | bytes 2097152
  198.2 0.0 copy-done.3
  198.2 0.6 copy.19
  198.8 0.0 copy-done.1
  198.8 0.0 copy-start.2
  198.8 0.9 copy.20
  199.7 0.4 copy-done.2
  200.1 0.8 copy.21
Async XLA Ops:
  0.6 0.7 copy-start.4
  2.2 0.8 copy-start
  195.8 2.4 %copy-start.3 = (f32[2,1024]{1,0:T(2,128)S(1)}, f32[2,1024]{1,0:T(2,128)}, u32[]{:S(2)}) copy-start(f32[2,1024]{1,0:T(2,128)} %get-tuple-element.9) | copy-start | bytes 24580
  195.8 3.0 %copy-start.1 = (bf16[2,2,224,512]{3,2,1,0:T(8,128)(2,1)S(1)}, bf16[2,2,224,512]{3,2,1,0:T(8,128)(2,1)}, u32[]{:S(2)}) copy-start(bf16[2,2,224,512]{3,2,1,0:T(8,128)(2,1)} %get-tuple-element.18) | copy-start | bytes 2752516
  198.8 1.3 copy-start.2

commit v2 on v1

v2 whole, which is shorter than its diff:
```python
import functools

import jax
import jax.numpy as jnp
from jax import lax
from jax.experimental import pallas as pl
from jax.experimental.pallas import tpu as pltpu
from jax.sharding import PartitionSpec as P

H = 8
NX = 4
NH = 2
MESH = pl.DeviceIdType.MESH
F32 = jnp.float32
BF16 = jnp.bfloat16
BLOCKS = 4
FLIP = True
GRID = {16: (4, 2, 2), 2: (1, 1, 2)}


def dot_nn(a, b):
    return lax.dot_general(a, b, (((1,), (0,)), ((), ())), preferred_element_type=F32)


def dot_nt(a, b):
    return lax.dot_general(a, b, (((1,), (1,)), ((), ())), preferred_element_type=F32)


def dot_tn(a, b):
    return lax.dot_general(a, b, (((0,), (0,)), ((), ())), preferred_element_type=F32)


def send_order(nz, ny, nc):
    order = []
    for dc in range(nc):
        for s in range(nz):
            for dy in range(ny):
                order.append((dy, (3 * dy + s) % nz, dc))
    return order


def kernel(
    dims,
    tok,
    cot,
    place_row,
    prob_row,
    place_col,
    w_in,
    w_out,
    gtok,
    gprob,
    gin,
    gout,
    rows_buf,
    xs_send,
    xs_all,
    wall,
    acts,
    dx,
    racc,
    rs_far,
    rs_sum,
    rs_dir,
    back,
    r_send,
    r_back,
    w_ssem,
    w_rsem,
    x_ssem,
    x_rsem,
    g_ssem,
    g_rsem,
    d_ssem,
    d_rsem,
    r_ssem,
    r_rsem,
):
    ng, toks, d, fs, cap = dims
    nz, nyl, nc = GRID[ng]
    ny = NH * nyl
    peers = NH * ng
    rows = toks * H
    slots = peers * cap
    half = fs // 2
    fc = NH * fs
    jb = slots // BLOCKS
    per = peers // BLOCKS
    order = send_order(nz, ny, nc)

    dp = lax.axis_index("dp")
    g = lax.axis_index("expert")
    x = dp // NH
    h = dp % NH
    core = g % nc
    y = h * nyl + (g // nc) % nyl
    z = g // (nc * nyl)
    right = (x + 1) % NX
    left = (x + 3) % NX
    far = (x + 2) % NX
    other = 1 - h
    me = g * NH + h

    def place_of(ty, tz, tc):
        return ((tz * nyl + ty % nyl) * nc + tc) * NH + ty // nyl

    def target(t):
        dy, dz, dc = order[t]
        sign = 1 - 2 * core if FLIP else 1
        return place_of(
            (y + sign * dy + ny) % ny, (z + sign * dz + nz) % nz, (core + dc) % nc
        )

    def source(t):
        dy, dz, dc = order[t]
        tc = (core + dc) % nc
        sign = 1 - 2 * tc if FLIP else 1
        return place_of((y - sign * dy + ny) % ny, (z - sign * dz + nz) % nz, tc)

    def device(u):
        return (x * NH + u % NH, u // NH)

    def remote(src, dst, ssem, rsem, to):
        return pltpu.make_async_remote_copy(
            src_ref=src,
            dst_ref=dst,
            send_sem=ssem,
            recv_sem=rsem,
            device_id=to,
            device_id_type=MESH,
        )

    barrier = pltpu.get_barrier_semaphore()
    to_right = (right * NH + h, g)
    to_left = (left * NH + h, g)
    to_partner = (x * NH + other, g)
    for t in range(1, peers):
        pl.semaphore_signal(barrier, inc=1, device_id=device(target(t)), device_id_type=MESH)
    for to in (to_right, to_left):
        pl.semaphore_signal(barrier, inc=1, device_id=to, device_id_type=MESH)

    for n in range(H):
        rows_buf[n * toks : (n + 1) * toks, :] = tok[:, n * d : (n + 1) * d]
        rows_buf[rows + n * toks : rows + (n + 1) * toks, :] = cot[:, n * d : (n + 1) * d]
    pl.semaphore_wait(barrier, peers + 1)

    def wcopy(k, src, dst, to):
        return remote(src, dst, w_ssem.at[k], w_rsem.at[k], to)

    first = [
        wcopy(0, w_in.at[other], wall.at[x, pl.ds(0, 2), h], to_partner),
        wcopy(1, w_out.at[other], wall.at[x, 2, h], to_partner),
        wcopy(2, w_in.at[h], wall.at[x, pl.ds(0, 2), h], to_right),
        wcopy(3, w_out.at[h], wall.at[x, 2, h], to_right),
        wcopy(4, w_in.at[h], wall.at[x, pl.ds(0, 2), h], to_left),
        wcopy(5, w_out.at[h], wall.at[x, 2, h], to_left),
    ]
    for c in first:
        c.start()

    pairs = nz * nyl
    width = min(2, pairs)
    span = NH * cap

    def xs_copy(t):
        u = target(t)
        return remote(xs_send.at[u], xs_all.at[t], x_ssem.at[t], x_rsem.at[t], device(u))

    for dc in range(nc):
        cc = (core + dc) % nc

        def dispatch(i, carry):
            row = lax.broadcasted_iota(jnp.int32, (width * span, rows), 0)
            ids = row + ((i * width * nc + cc) * span)
            if width == 2:
                ids = ids + jnp.where(row >= span, (nc - 1) * span, 0)
            hit0 = place_row[0:1, :] == ids
            hit1 = place_row[1:2, :] == ids
            one = jnp.where(hit0 | hit1, 1.0, 0.0).astype(BF16)
            wgt = jnp.where(hit0, prob_row[0:1, :], jnp.where(hit1, prob_row[1:2, :], 0.0))
            xr = dot_nn(one, rows_buf[0:rows, :]).astype(BF16)
            sr = dot_nn(wgt.astype(BF16), rows_buf[rows : 2 * rows, :]).astype(BF16)
            for j in range(width):
                e0 = ((i * width + j) * nc + cc) * NH
                for k in range(NH):
                    at = (j * NH + k) * cap
                    xs_send[e0 + k, 0] = xr[at : at + cap, :]
                    xs_send[e0 + k, 1] = sr[at : at + cap, :]
            return carry

        lax.fori_loop(0, pairs // width, dispatch, 0)
        for t in range(1, peers):
            if order[t][2] == dc:
                xs_copy(t).start()

    wall[x, 0:2, h] = w_in[h]
    wall[x, 2, h] = w_out[h]
    xs_all[0] = xs_send[me]
    racc[...] = jnp.zeros_like(racc)
    dx[...] = jnp.zeros_like(dx)

    def wforward(k, slot, part_rows, plane, to):
        ref = wall.at[slot, pl.ds(0, 3), plane, part_rows]
        return wcopy(k, ref, ref, to)

    top, bottom, full = pl.ds(0, half), pl.ds(half, half), pl.ds(0, fs)

    def xs_wait(i):
        for t in range(max(1, i * per), (i + 1) * per):
            xs_copy(t).wait_recv()

    def block(xc, i):
        at = pl.ds(pl.multiple_of(i * jb, jb), jb)
        some = pl.ds(i * per, per)
        xb = xs_all[some, 0].reshape(jb, d)
        sb = xs_all[some, 1].reshape(jb, d)
        wg = wall[xc, 0].reshape(fc, d)
        wu = wall[xc, 1].reshape(fc, d)
        wo = wall[xc, 2].reshape(fc, d)
        gate = dot_nt(wg, xb)
        up = dot_nt(wu, xb)
        dh = dot_nt(wo, sb)
        sg = 0.5 * jnp.tanh(0.5 * gate) + 0.5
        a = gate * sg
        du = dh * a
        dg = dh * up * (sg + a * (1.0 - sg))
        dgb = dg.astype(BF16)
        dub = du.astype(BF16)
        acts[xc, 0, :, :, at] = dgb.reshape(NH, fs, jb)
        acts[xc, 1, :, :, at] = dub.reshape(NH, fs, jb)
        acts[xc, 2, :, :, at] = (a * up).astype(BF16).reshape(NH, fs, jb)
        racc[:, at] += jnp.sum((du * up).reshape(fc // 8, 8, jb), axis=0)
        dx[at, :] += dot_tn(dgb, wg) + dot_tn(dub, wu)

    def sweep(count, xc_of, i_of):
        def step(n, carry):
            block(xc_of(n), i_of(n))
            return carry

        lax.fori_loop(0, count, step, 0)

    first[2].wait_recv()
    first[3].wait_recv()
    f6 = wforward(6, left, top, h, to_right)
    f6.start()
    first[4].wait_recv()
    first[5].wait_recv()
    f7 = wforward(7, right, bottom, h, to_left)
    f7.start()
    first[0].wait_recv()
    first[1].wait_recv()
    f8 = wforward(8, x, full, other, to_right)
    f8.start()
    f9 = wforward(9, x, full, other, to_left)
    f9.start()
    xs_wait(0)
    sweep(1, lambda n: x, lambda n: n * 0)
    f8.wait_recv()
    f10 = wforward(10, left, top, other, to_right)
    f10.start()
    f9.wait_recv()
    f11 = wforward(11, right, bottom, other, to_left)
    f11.start()
    sweep(2, lambda n: (x + 1 + 2 * n) % NX, lambda n: n * 0)
    xs_wait(1)
    sweep(3, lambda n: (x + jnp.where(n == 2, 3, n)) % NX, lambda n: n * 0 + 1)
    for c in (f6, f7, f10, f11):
        c.wait_recv()
    sweep(2, lambda n: far, lambda n: n)
    xs_wait(2)
    sweep(4, lambda n: (x + 2 + n) % NX, lambda n: n * 0 + 2)
    xs_wait(3)

    def give(i):
        for k in range(per):
            t = i * per + k
            dst = rows_buf.at[pl.ds(t * cap, cap)]
            if t:
                u = source(t)
                remote(dst, back.at[me], d_ssem.at[t], d_rsem.at[me], device(u)).start()
                remote(r_send.at[t], r_back.at[me], r_ssem.at[t], r_rsem.at[me], device(u)).start()
            else:
                back[me] = rows_buf[0:cap, :]
                r_back[me] = r_send[0]

    def finish(i):
        rows_buf[i * jb : (i + 1) * jb, :] = dx[i * jb : (i + 1) * jb, :].astype(BF16)
        r_row = jnp.sum(racc[:, i * jb : (i + 1) * jb], axis=0, keepdims=True)
        for k in range(per):
            v = r_row[:, k * cap : (k + 1) * cap]
            r_send[i * per + k] = jnp.broadcast_to(jnp.concatenate([v, v], axis=1), (8, 128))

    planes = (other, h)

    def gcopy(k, src, dst, to):
        return remote(src, dst, g_ssem.at[k], g_rsem.at[k], to)

    def piece(xc, part_rows, plane):
        return acts.at[xc, pl.ds(0, 3), plane, part_rows, pl.ds(0, d)]

    far_right = [gcopy(p, piece(far, top, planes[p]), rs_far.at[0, p], to_right) for p in (0, 1)]
    far_left = [
        gcopy(2 + p, piece(far, bottom, planes[p]), rs_far.at[1, p], to_left) for p in (0, 1)
    ]
    dir_right = [
        gcopy(4 + p, piece(right, bottom, planes[p]), rs_dir.at[0, p], to_right) for p in (0, 1)
    ]
    dir_left = [
        gcopy(6 + p, piece(left, top, planes[p]), rs_dir.at[1, p], to_left) for p in (0, 1)
    ]
    sum_right = [
        gcopy(8 + p, piece(right, top, planes[p]), rs_sum.at[0, p], to_right) for p in (0, 1)
    ]
    sum_left = [
        gcopy(10 + p, piece(left, bottom, planes[p]), rs_sum.at[1, p], to_left) for p in (0, 1)
    ]

    def weight_grads(xc):
        xa = xs_all[:, 0].reshape(slots, d)
        sa = xs_all[:, 1].reshape(slots, d)
        for m, against in ((0, xa), (1, xa), (2, sa)):
            grad = dot_nn(acts[xc, m].reshape(fc, slots), against)
            acts[xc, m, :, :, 0:d] = grad.astype(BF16).reshape(NH, fs, d)

    def add_far(side, p):
        xc, part_rows = (right, top) if side == 0 else (left, bottom)
        for m in range(3):
            mine = acts[xc, m, planes[p], part_rows, 0:d].astype(F32)
            acts[xc, m, planes[p], part_rows, 0:d] = (
                rs_far[side, p, m].astype(F32) + mine
            ).astype(BF16)

    def last(n, carry):
        xc = (x + jnp.where(n == 0, 2, jnp.where(n == 1, 1, jnp.where(n == 2, 3, 0)))) % NX
        block(xc, BLOCKS - 1)

        @pl.when(n == 3)
        def _():
            finish(3)
            give(3)

        weight_grads(xc)

        @pl.when(n == 0)
        def _():
            for p in (0, 1):
                far_right[p].start()
                far_left[p].start()
            for i in range(3):
                finish(i)
                give(i)

        @pl.when(n == 1)
        def _():
            dir_right[0].start()

        @pl.when(n == 2)
        def _():
            dir_left[0].start()
            far_right[0].wait_recv()
            add_far(0, 0)
            sum_right[0].start()
            dir_right[1].start()
            far_left[0].wait_recv()
            add_far(1, 0)
            sum_left[0].start()
            dir_left[1].start()

        return carry

    lax.fori_loop(0, NX, last, 0)
    far_right[1].wait_recv()
    add_far(0, 1)
    sum_right[1].start()
    far_left[1].wait_recv()
    add_far(1, 1)
    sum_left[1].start()

    def total(m, p, lower):
        mine = acts[x, m, planes[p], pl.ds(half if lower else 0, half), 0:d].astype(F32)
        if lower:
            got = rs_dir[0, p, m].astype(F32) + rs_sum[1, p, m].astype(F32)
        else:
            got = rs_dir[1, p, m].astype(F32) + rs_sum[0, p, m].astype(F32)
        return (mine + got).astype(BF16)

    for c in (dir_right, dir_left, sum_right, sum_left):
        c[0].wait_recv()
    for m in range(3):
        acts[x, m, other, 0:half, 0:d] = total(m, 0, False)
        acts[x, m, other, half:fs, 0:d] = total(m, 0, True)
    swap_in = gcopy(12, acts.at[x, pl.ds(0, 2), other, full, pl.ds(0, d)], gin.at[h], to_partner)
    swap_out = gcopy(13, acts.at[x, 2, other, full, pl.ds(0, d)], gout.at[h], to_partner)
    swap_in.start()
    swap_out.start()

    for t in range(1, peers):
        u = target(t)
        dst = rows_buf.at[pl.ds(0, cap)]
        remote(dst, back.at[u], d_ssem.at[t], d_rsem.at[u], device(u)).wait_recv()
        remote(r_send.at[0], r_back.at[u], r_ssem.at[t], r_rsem.at[u], device(u)).wait_recv()
    for n in range(H):
        pc = place_col[n * toks : (n + 1) * toks, :]
        ids = lax.broadcasted_iota(jnp.int32, (toks, slots), 1)
        one = jnp.where((pc[:, 0:1] == ids) | (pc[:, 1:2] == ids), 1.0, 0.0).astype(BF16)
        gtok[:, n * d : (n + 1) * d] = dot_nn(one, back[...].reshape(slots, d)).astype(BF16)

    r_mine = r_back[:, 0, :]
    for k in range(2):
        pr = place_row[k : k + 1, :]
        expert = lax.shift_right_logical(pr, cap.bit_length() - 1)
        slot = lax.bitwise_and(pr, cap - 1)
        pick = jnp.where(lax.broadcasted_iota(jnp.int32, (peers, rows), 0) == expert, 1.0, 0.0)
        table = lax.dot_general(
            r_mine,
            pick,
            (((0,), (0,)), ((), ())),
            precision=lax.Precision.HIGHEST,
            preferred_element_type=F32,
        )
        lanes = lax.broadcasted_iota(jnp.int32, (128, rows), 0)
        value = jnp.sum(jnp.where(lanes == slot, table, 0.0), axis=0, keepdims=True)
        gprob[k : k + 1, :] = value / prob_row[k : k + 1, :]

    for c in (dir_right, dir_left, sum_right, sum_left):
        c[1].wait_recv()
    for m in range(2):
        gin[h, m, 0:half] = total(m, 1, False)
        gin[h, m, half:fs] = total(m, 1, True)
    gout[h, 0:half] = total(2, 1, False)
    gout[h, half:fs] = total(2, 1, True)

    for c in first + [f6, f7, f8, f9, f10, f11]:
        c.wait_send()
    for c in (far_right, far_left, dir_right, dir_left, sum_right, sum_left):
        c[0].wait_send()
        c[1].wait_send()
    for t in range(1, peers):
        xs_copy(t).wait_send()
        dst = rows_buf.at[pl.ds(0, cap)]
        remote(dst, back.at[0], d_ssem.at[t], d_rsem.at[0], device(source(t))).wait_send()
        remote(r_send.at[0], r_back.at[0], r_ssem.at[t], r_rsem.at[0], device(source(t))).wait_send()
    swap_in.wait()
    swap_out.wait()


def body(tokens, cotangent, expert_ids, slot_ids, route_probs, weights_in, weights_out):
    ng = lax.axis_size("expert")
    toks = tokens.shape[0]
    d = tokens.shape[1] // H
    fs = weights_in.shape[2]
    peers = NH * ng
    rows = toks * H
    cap = rows * 2 // peers
    slots = peers * cap
    half = fs // 2
    fc = NH * fs

    place = jnp.transpose(expert_ids * cap + slot_ids, (2, 1, 0)).reshape(2, rows)
    probs = jnp.transpose(route_probs, (2, 1, 0)).reshape(2, rows).astype(F32)
    place_col = jnp.transpose(place, (1, 0))

    vmem = pl.BlockSpec(memory_space=pltpu.VMEM)
    dma = pltpu.SemaphoreType.DMA
    gtok, gprob, gin, gout = pl.pallas_call(
        functools.partial(kernel, (ng, toks, d, fs, cap)),
        out_shape=(
            jax.ShapeDtypeStruct((toks, H * d), BF16),
            jax.ShapeDtypeStruct((2, rows), F32),
            jax.ShapeDtypeStruct((2, 2, fs, d), BF16),
            jax.ShapeDtypeStruct((2, fs, d), BF16),
        ),
        in_specs=[vmem] * 7,
        out_specs=(vmem,) * 4,
        scratch_shapes=[
            pltpu.VMEM((2 * rows, d), BF16),
            pltpu.VMEM((peers, 2, cap, d), BF16),
            pltpu.VMEM((peers, 2, cap, d), BF16),
            pltpu.VMEM((NX, 3, NH, fs, d), BF16),
            pltpu.VMEM((NX, 3, NH, fs, slots), BF16),
            pltpu.VMEM((slots, d), F32),
            pltpu.VMEM((8, slots), F32),
            pltpu.VMEM((2, 2, 3, half, d), BF16),
            pltpu.VMEM((2, 2, 3, half, d), BF16),
            pltpu.VMEM((2, 2, 3, half, d), BF16),
            pltpu.VMEM((peers, cap, d), BF16),
            pltpu.VMEM((peers, 8, 128), F32),
            pltpu.VMEM((peers, 8, 128), F32),
            dma((12,)),
            dma((12,)),
            dma((peers,)),
            dma((peers,)),
            dma((14,)),
            dma((14,)),
            dma((peers,)),
            dma((peers,)),
            dma((peers,)),
            dma((peers,)),
        ],
        compiler_params=pltpu.CompilerParams(
            collective_id=0, has_side_effects=True, vmem_limit_bytes=67_000_000
        ),
        name="moe_backward",
    )(tokens, cotangent, place, probs, place_col, weights_in, weights_out)
    grad_probs = jnp.transpose(gprob.reshape(2, H, toks), (2, 1, 0))
    return gtok, grad_probs, gin, gout


def solution(mesh):
    return jax.shard_map(
        body,
        mesh=mesh,
        in_specs=(
            P(("dp", "expert"), None),
            P(("dp", "expert"), None),
            P(("dp", "expert"), None, None),
            P(("dp", "expert"), None, None),
            P(("dp", "expert"), None, None),
            P("expert", None, "dp", None),
            P("expert", "dp", None),
        ),
        out_specs=(
            P(("dp", "expert"), None),
            P(("dp", "expert"), None, None),
            P("expert", None, "dp", None),
            P("expert", "dp", None),
        ),
        check_vma=False,
    )
```

time: 201 us -> 139 us (0.69)
  the two profiles are of different devices: /device:TPU:97 before, /device:TPU:0 now
where the time goes in v2:
time: 139 us
  Pallas kernels  130 us (94%)
  local copies, waits for them, and re-layouts  6.87 us (5%)
    pallas_call x1, Pallas kernels, body(): pl.pallas_call(functools.partial(kernel, (ng, toks, d, fs, cap)), out_sha...  130 us
    unnamed x14, local copies, waits for them, and re-layouts  5.86 us

profile of v2, /device:TPU:0, one launch (start us, length us, event | category | flops | bytes accessed | tf_op | source)
XLA Modules:
  0.0 139.2 jit_solution(12425734632599928025)
XLA Ops:
  0.6 0.0 copy-start.4
  0.6 0.7 add_bitcast_fusion
  1.4 0.0 copy-done.4
  1.4 0.6 convert_bitcast_fusion.prob_row
  2.0 0.2 copy.11
  2.2 0.0 copy-start
  2.2 0.8 copy-done
  3.0 0.8 copy.12.place_row
  3.8 130.3 %moe_backward.1 = (bf16[128,4096]{1,0:T(8,128)(2,1)}, f32[2,1024]{1,0:T(2,128)}, bf16[2,2,224,512]{3,2,1,0:T(8,128)(2,1)}, bf16[2,224,512]{2,1,0:T(8,128)(2,1)}) custom-call(bf16[128,4096]{1,0:T(8,128)(2,1)} %tok.1, bf16[128,4096]{1,0:T(8,128)(2,1)} %cot.1, s32[2,1024]{1,0:T(2,128)} %copy.12.place_row, f32[2,1024]{1,0:T(2,128)} %convert_bitcast_fusion.prob_row, ...), custom_call_target="tpu_custom_call" | custom-call | tf_op jit(solution)/shard_map/moe_backward/pallas_call | solution.py:465
  134.1 0.0 copy-start.3
  134.1 0.0 copy-start.1
  134.1 2.4 %copy.18 = bf16[128,4096]{1,0:T(8,128)(2,1)} copy(bf16[128,4096]{1,0:T(8,128)(2,1)} %get-tuple-element.16) | data formatting | bytes 2097152
  136.5 0.0 copy-done.3
  136.5 0.6 copy.19
  137.1 0.0 copy-done.1
  137.1 0.0 copy-start.2
  137.1 0.9 copy.20
  138.0 0.4 copy-done.2
  138.4 0.8 copy.21
Async XLA Ops:
  0.6 0.7 copy-start.4
  2.2 0.8 copy-start
  134.1 2.4 %copy-start.3 = (f32[2,1024]{1,0:T(2,128)S(1)}, f32[2,1024]{1,0:T(2,128)}, u32[]{:S(2)}) copy-start(f32[2,1024]{1,0:T(2,128)} %get-tuple-element.9) | copy-start | bytes 24580
  134.1 3.0 %copy-start.1 = (bf16[2,2,224,512]{3,2,1,0:T(8,128)(2,1)S(1)}, bf16[2,2,224,512]{3,2,1,0:T(8,128)(2,1)}, u32[]{:S(2)}) copy-start(bf16[2,2,224,512]{3,2,1,0:T(8,128)(2,1)} %get-tuple-element.18) | copy-start | bytes 2752516
  137.1 1.3 copy-start.2

commit v3 on v2

--- a/solution.py
+++ b/solution.py
@@ -43,15 +43,19 @@
     dims,
     tok,
     cot,
-    place_row,
-    prob_row,
-    place_col,
+    ids_in,
+    slots_in,
+    probs_in,
     w_in,
     w_out,
     gtok,
     gprob,
     gin,
     gout,
+    place_row,
+    prob_row,
+    gtok_buf,
+    far_acc,
     rows_buf,
     xs_send,
     xs_all,
@@ -75,6 +79,7 @@
     d_rsem,
     r_ssem,
     r_rsem,
+    l_sem,
 ):
     ng, toks, d, fs, cap = dims
     nz, nyl, nc = GRID[ng]
@@ -139,9 +144,21 @@
     for to in (to_right, to_left):
         pl.semaphore_signal(barrier, inc=1, device_id=to, device_id_type=MESH)
 
-    for n in range(H):
-        rows_buf[n * toks : (n + 1) * toks, :] = tok[:, n * d : (n + 1) * d]
-        rows_buf[rows + n * toks : rows + (n + 1) * toks, :] = cot[:, n * d : (n + 1) * d]
+    local = []
+    for k, src in enumerate((tok, cot)):
+        for n in range(H):
+            dst = rows_buf.at[pl.ds((k * H + n) * toks, toks)]
+            local.append((src.at[:, pl.ds(n * d, d)], dst))
+    local.append((w_in.at[h], wall.at[x, pl.ds(0, 2), h]))
+    local.append((w_out.at[h], wall.at[x, 2, h]))
+    local = [pltpu.make_async_copy(a, b, l_sem.at[n]) for n, (a, b) in enumerate(local)]
+    for c in local:
+        c.start()
+    place = ids_in[...] * cap + slots_in[...]
+    probs = probs_in[...].astype(F32)
+    for k in range(2):
+        place_row[k : k + 1, :] = jnp.concatenate([place[n, k : k + 1] for n in range(H)], axis=1)
+        prob_row[k : k + 1, :] = jnp.concatenate([probs[n, k : k + 1] for n in range(H)], axis=1)
     pl.semaphore_wait(barrier, peers + 1)
 
     def wcopy(k, src, dst, to):
@@ -157,6 +174,9 @@
     ]
     for c in first:
         c.start()
+
+    for c in local:
+        c.wait()
 
     pairs = nz * nyl
     width = min(2, pairs)
@@ -193,8 +213,6 @@
             if order[t][2] == dc:
                 xs_copy(t).start()
 
-    wall[x, 0:2, h] = w_in[h]
-    wall[x, 2, h] = w_out[h]
     xs_all[0] = xs_send[me]
     racc[...] = jnp.zeros_like(racc)
     dx[...] = jnp.zeros_like(dx)
@@ -269,6 +287,13 @@
     sweep(2, lambda n: far, lambda n: n)
     xs_wait(2)
     sweep(4, lambda n: (x + 2 + n) % NX, lambda n: n * 0 + 2)
+
+    before = slots - jb
+    for m in range(3):
+        far_acc[m] = dot_nn(
+            acts[far, m, :, :, 0:before].reshape(fc, before),
+            xs_all[0 : peers - per, m // 2].reshape(before, d),
+        )
     xs_wait(3)
 
     def give(i):
@@ -330,31 +355,36 @@
                 rs_far[side, p, m].astype(F32) + mine
             ).astype(BF16)
 
+    block(far, BLOCKS - 1)
+    for m in range(3):
+        grad = far_acc[m] + dot_nn(
+            acts[far, m, :, :, before:slots].reshape(fc, jb),
+            xs_all[peers - per : peers, m // 2].reshape(jb, d),
+        )
+        acts[far, m, :, :, 0:d] = grad.astype(BF16).reshape(NH, fs, d)
+    for p in (0, 1):
+        far_right[p].start()
+        far_left[p].start()
+    for i in range(BLOCKS - 1):
+        finish(i)
+        give(i)
+
     def last(n, carry):
-        xc = (x + jnp.where(n == 0, 2, jnp.where(n == 1, 1, jnp.where(n == 2, 3, 0)))) % NX
+        xc = (x + jnp.where(n == 0, 1, jnp.where(n == 1, 3, 0))) % NX
         block(xc, BLOCKS - 1)
 
-        @pl.when(n == 3)
+        @pl.when(n == 2)
         def _():
-            finish(3)
-            give(3)
+            finish(BLOCKS - 1)
+            give(BLOCKS - 1)
 
         weight_grads(xc)
 
         @pl.when(n == 0)
         def _():
-            for p in (0, 1):
-                far_right[p].start()
-                far_left[p].start()
-            for i in range(3):
-                finish(i)
-                give(i)
+            dir_right[0].start()
 
         @pl.when(n == 1)
-        def _():
-            dir_right[0].start()
-
-        @pl.when(n == 2)
         def _():
             dir_left[0].start()
             far_right[0].wait_recv()
@@ -368,7 +398,7 @@
 
         return carry
 
-    lax.fori_loop(0, NX, last, 0)
+    lax.fori_loop(0, NX - 1, last, 0)
     far_right[1].wait_recv()
     add_far(0, 1)
     sum_right[1].start()
@@ -399,11 +429,19 @@
         dst = rows_buf.at[pl.ds(0, cap)]
         remote(dst, back.at[u], d_ssem.at[t], d_rsem.at[u], device(u)).wait_recv()
         remote(r_send.at[0], r_back.at[u], r_ssem.at[t], r_rsem.at[u], device(u)).wait_recv()
+    flat = jnp.concatenate(
+        [place_row[k : k + 1, n * toks : (n + 1) * toks] for n in range(H) for k in range(2)],
+        axis=0,
+    )
+    cols = jnp.transpose(flat.astype(F32), (1, 0)).astype(jnp.int32)
+    ids = lax.broadcasted_iota(jnp.int32, (toks, slots), 1)
     for n in range(H):
-        pc = place_col[n * toks : (n + 1) * toks, :]
-        ids = lax.broadcasted_iota(jnp.int32, (toks, slots), 1)
-        one = jnp.where((pc[:, 0:1] == ids) | (pc[:, 1:2] == ids), 1.0, 0.0).astype(BF16)
-        gtok[:, n * d : (n + 1) * d] = dot_nn(one, back[...].reshape(slots, d)).astype(BF16)
+        hit = (cols[:, 2 * n : 2 * n + 1] == ids) | (cols[:, 2 * n + 1 : 2 * n + 2] == ids)
+        one = jnp.where(hit, 1.0, 0.0).astype(BF16)
+        grad = dot_nn(one, back[...].reshape(slots, d))
+        gtok_buf[:, n * d : (n + 1) * d] = grad.astype(BF16)
+    tok_out = pltpu.make_async_copy(gtok_buf, gtok, l_sem.at[2 * H + 2])
+    tok_out.start()
 
     r_mine = r_back[:, 0, :]
     for k in range(2):
@@ -420,7 +458,9 @@
         )
         lanes = lax.broadcasted_iota(jnp.int32, (128, rows), 0)
         value = jnp.sum(jnp.where(lanes == slot, table, 0.0), axis=0, keepdims=True)
-        gprob[k : k + 1, :] = value / prob_row[k : k + 1, :]
+        ratio = value / prob_row[k : k + 1, :]
+        for n in range(H):
+            gprob[n, k : k + 1, :] = ratio[:, n * toks : (n + 1) * toks]
 
     for c in (dir_right, dir_left, sum_right, sum_left):
         c[1].wait_recv()
@@ -430,6 +470,7 @@
     gout[h, 0:half] = total(2, 1, False)
     gout[h, half:fs] = total(2, 1, True)
 
+    tok_out.wait()
     for c in first + [f6, f7, f8, f9, f10, f11]:
         c.wait_send()
     for c in (far_right, far_left, dir_right, dir_left, sum_right, sum_left):
@@ -444,6 +485,29 @@
     swap_out.wait()
 
 
+def copy_kernel(*refs):
+    ins, outs, bufs, (in_sem, out_sem) = refs[0:4], refs[4:8], refs[8:12], refs[12:14]
+    count = ins[0].shape[0] // 4
+    parts = [(0, pl.ds(k * count, count)) for k in range(4)]
+    parts += [(2, pl.ds(0, 1)), (2, pl.ds(1, 1)), (3, pl.ds(0, 1)), (3, pl.ds(1, 1))]
+    parts += [(1, pl.ds(0, ins[1].shape[0]))]
+    moves = []
+    for n, (a, at) in enumerate(parts):
+        moves.append(
+            (
+                pltpu.make_async_copy(ins[a].at[at], bufs[a].at[at], in_sem.at[n]),
+                pltpu.make_async_copy(bufs[a].at[at], outs[a].at[at], out_sem.at[n]),
+            )
+        )
+    for into, _ in moves:
+        into.start()
+    for into, out in moves:
+        into.wait()
+        out.start()
+    for _, out in moves:
+        out.wait()
+
+
 def body(tokens, cotangent, expert_ids, slot_ids, route_probs, weights_in, weights_out):
     ng = lax.axis_size("expert")
     toks = tokens.shape[0]
@@ -456,23 +520,24 @@
     half = fs // 2
     fc = NH * fs
 
-    place = jnp.transpose(expert_ids * cap + slot_ids, (2, 1, 0)).reshape(2, rows)
-    probs = jnp.transpose(route_probs, (2, 1, 0)).reshape(2, rows).astype(F32)
-    place_col = jnp.transpose(place, (1, 0))
-
     vmem = pl.BlockSpec(memory_space=pltpu.VMEM)
+    anywhere = pl.BlockSpec(memory_space=pl.ANY)
     dma = pltpu.SemaphoreType.DMA
     gtok, gprob, gin, gout = pl.pallas_call(
         functools.partial(kernel, (ng, toks, d, fs, cap)),
         out_shape=(
             jax.ShapeDtypeStruct((toks, H * d), BF16),
-            jax.ShapeDtypeStruct((2, rows), F32),
+            jax.ShapeDtypeStruct((H, 2, toks), F32),
             jax.ShapeDtypeStruct((2, 2, fs, d), BF16),
             jax.ShapeDtypeStruct((2, fs, d), BF16),
         ),
-        in_specs=[vmem] * 7,
-        out_specs=(vmem,) * 4,
+        in_specs=[anywhere] * 2 + [vmem] * 3 + [anywhere] * 2,
+        out_specs=(anywhere, vmem, vmem, vmem),
         scratch_shapes=[
+            pltpu.VMEM((2, rows), jnp.int32),
+            pltpu.VMEM((2, rows), F32),
+            pltpu.VMEM((toks, H * d), BF16),
+            pltpu.VMEM((3, fc, d), F32),
             pltpu.VMEM((2 * rows, d), BF16),
             pltpu.VMEM((peers, 2, cap, d), BF16),
             pltpu.VMEM((peers, 2, cap, d), BF16),
@@ -496,14 +561,31 @@
             dma((peers,)),
             dma((peers,)),
             dma((peers,)),
+            dma((2 * H + 3,)),
         ],
         compiler_params=pltpu.CompilerParams(
             collective_id=0, has_side_effects=True, vmem_limit_bytes=67_000_000
         ),
         name="moe_backward",
-    )(tokens, cotangent, place, probs, place_col, weights_in, weights_out)
-    grad_probs = jnp.transpose(gprob.reshape(2, H, toks), (2, 1, 0))
-    return gtok, grad_probs, gin, gout
+    )(
+        tokens,
+        cotangent,
+        jnp.transpose(expert_ids, (1, 2, 0)),
+        jnp.transpose(slot_ids, (1, 2, 0)),
+        jnp.transpose(route_probs, (1, 2, 0)),
+        weights_in,
+        weights_out,
+    )
+    gtok, gprob, gin, gout = pl.pallas_call(
+        copy_kernel,
+        out_shape=tuple(jax.ShapeDtypeStruct(a.shape, a.dtype) for a in (gtok, gprob, gin, gout)),
+        in_specs=[anywhere] * 4,
+        out_specs=(anywhere,) * 4,
+        scratch_shapes=[pltpu.VMEM(a.shape, a.dtype) for a in (gtok, gprob, gin, gout)]
+        + [dma((10,)), dma((10,))],
+        name="results",
+    )(gtok, gprob, gin, gout)
+    return gtok, jnp.transpose(gprob, (2, 0, 1)), gin, gout
 
 
 def solution(mesh):

time: 139 us -> 130 us (0.935)
  local copies, waits for them, and re-layouts: 6.87 us -> 0 us
    unnamed x14 -> x0, local copies, waits for them, and re-layouts: 5.86 us -> none
    pallas_call x1, Pallas kernels: 130 us -> 126 us  [body(): pl.pallas_call(functools.partial(kernel, (ng, toks, d, fs, cap)), out_sha...]
    pallas_call x0 -> x1, Pallas kernels: none -> 2.58 us  [body(): pl.pallas_call(copy_kernel, out_shape=tuple((jax.ShapeDtypeStruct(a.shape...]
where the time goes in v3:
time: 130 us
  Pallas kernels  129 us (99%)
    pallas_call x1, Pallas kernels, body(): pl.pallas_call(functools.partial(kernel, (ng, toks, d, fs, cap)), out_sha...  126 us

profile of v3, /device:TPU:0, one launch (start us, length us, event | category | flops | bytes accessed | tf_op | source)
XLA Modules:
  0.0 129.6 jit_solution(6269003238709718816)
XLA Ops:
  0.6 126.2 %moe_backward.1 = (bf16[128,4096]{1,0:T(8,128)(2,1)}, f32[8,2,128]{2,1,0:T(2,128)}, bf16[2,2,224,512]{3,2,1,0:T(8,128)(2,1)}, bf16[2,224,512]{2,1,0:T(8,128)(2,1)}) custom-call(bf16[128,4096]{1,0:T(8,128)(2,1)} %tok.1, bf16[128,4096]{1,0:T(8,128)(2,1)} %cot.1, s32[8,2,128]{2,1,0:T(2,128)} %bitcast.4, s32[8,2,128]{2,1,0:T(2,128)} %bitcast.5, ...), custom_call_target="tpu_custom_call" | custom-call | tf_op jit(solution)/shard_map/moe_backward/pallas_call | solution.py:526
  126.9 2.6 %results.1 = (bf16[128,4096]{1,0:T(8,128)(2,1)}, f32[8,2,128]{2,1,0:T(2,128)}, bf16[2,2,224,512]{3,2,1,0:T(8,128)(2,1)}, bf16[2,224,512]{2,1,0:T(8,128)(2,1)}) custom-call(bf16[128,4096]{1,0:T(8,128)(2,1)} %get-tuple-element.12.refs_0_, f32[8,2,128]{2,1,0:T(2,128)} %get-tuple-element.13.refs_1_, bf16[2,2,224,512]{3,2,1,0:T(8,128)(2,1)} %get-tuple-element.14.refs_2_, ...), custom_call_target="tpu_custom_call" | custom-call | tf_op jit(solution)/shard_map/results/pallas_call | solution.py:579

commit v4 on v3

--- a/solution.py
+++ b/solution.py
@@ -54,7 +54,6 @@
     gout,
     place_row,
     prob_row,
-    gtok_buf,
     far_acc,
     rows_buf,
     xs_send,
@@ -223,11 +222,13 @@
 
     top, bottom, full = pl.ds(0, half), pl.ds(half, half), pl.ds(0, fs)
 
-    def xs_wait(i):
-        for t in range(max(1, i * per), (i + 1) * per):
+    def xs_wait(i, share=1):
+        count = per // share
+        for t in range(max(1, i * count), (i + 1) * count):
             xs_copy(t).wait_recv()
 
-    def block(xc, i):
+    def block(xc, i, share=1):
+        per, jb = peers // BLOCKS // share, slots // BLOCKS // share
         at = pl.ds(pl.multiple_of(i * jb, jb), jb)
         some = pl.ds(i * per, per)
         xb = xs_all[some, 0].reshape(jb, d)
@@ -294,8 +295,6 @@
             acts[far, m, :, :, 0:before].reshape(fc, before),
             xs_all[0 : peers - per, m // 2].reshape(before, d),
         )
-    xs_wait(3)
-
     def give(i):
         for k in range(per):
             t = i * per + k
@@ -355,7 +354,10 @@
                 rs_far[side, p, m].astype(F32) + mine
             ).astype(BF16)
 
-    block(far, BLOCKS - 1)
+    share = min(2, per)
+    for i in range((BLOCKS - 1) * share, BLOCKS * share):
+        xs_wait(i, share)
+        block(far, i, share)
     for m in range(3):
         grad = far_acc[m] + dot_nn(
             acts[far, m, :, :, before:slots].reshape(fc, jb),
@@ -439,9 +441,7 @@
         hit = (cols[:, 2 * n : 2 * n + 1] == ids) | (cols[:, 2 * n + 1 : 2 * n + 2] == ids)
         one = jnp.where(hit, 1.0, 0.0).astype(BF16)
         grad = dot_nn(one, back[...].reshape(slots, d))
-        gtok_buf[:, n * d : (n + 1) * d] = grad.astype(BF16)
-    tok_out = pltpu.make_async_copy(gtok_buf, gtok, l_sem.at[2 * H + 2])
-    tok_out.start()
+        gtok[:, n * d : (n + 1) * d] = grad.astype(BF16)
 
     r_mine = r_back[:, 0, :]
     for k in range(2):
@@ -462,6 +462,7 @@
         for n in range(H):
             gprob[n, k : k + 1, :] = ratio[:, n * toks : (n + 1) * toks]
 
+
     for c in (dir_right, dir_left, sum_right, sum_left):
         c[1].wait_recv()
     for m in range(2):
@@ -470,7 +471,6 @@
     gout[h, 0:half] = total(2, 1, False)
     gout[h, half:fs] = total(2, 1, True)
 
-    tok_out.wait()
     for c in first + [f6, f7, f8, f9, f10, f11]:
         c.wait_send()
     for c in (far_right, far_left, dir_right, dir_left, sum_right, sum_left):
@@ -486,26 +486,12 @@
 
 
 def copy_kernel(*refs):
-    ins, outs, bufs, (in_sem, out_sem) = refs[0:4], refs[4:8], refs[8:12], refs[12:14]
-    count = ins[0].shape[0] // 4
-    parts = [(0, pl.ds(k * count, count)) for k in range(4)]
-    parts += [(2, pl.ds(0, 1)), (2, pl.ds(1, 1)), (3, pl.ds(0, 1)), (3, pl.ds(1, 1))]
-    parts += [(1, pl.ds(0, ins[1].shape[0]))]
-    moves = []
-    for n, (a, at) in enumerate(parts):
-        moves.append(
-            (
-                pltpu.make_async_copy(ins[a].at[at], bufs[a].at[at], in_sem.at[n]),
-                pltpu.make_async_copy(bufs[a].at[at], outs[a].at[at], out_sem.at[n]),
-            )
-        )
-    for into, _ in moves:
-        into.start()
-    for into, out in moves:
-        into.wait()
-        out.start()
-    for _, out in moves:
-        out.wait()
+    ins, outs, sem = refs[0:4], refs[4:8], refs[8]
+    moves = [pltpu.make_async_copy(ins[n], outs[n], sem.at[n]) for n in range(4)]
+    for c in moves:
+        c.start()
+    for c in moves:
+        c.wait()
 
 
 def body(tokens, cotangent, expert_ids, slot_ids, route_probs, weights_in, weights_out):
@@ -526,17 +512,16 @@
     gtok, gprob, gin, gout = pl.pallas_call(
         functools.partial(kernel, (ng, toks, d, fs, cap)),
         out_shape=(
-            jax.ShapeDtypeStruct((toks, H * d), BF16),
-            jax.ShapeDtypeStruct((H, 2, toks), F32),
-            jax.ShapeDtypeStruct((2, 2, fs, d), BF16),
-            jax.ShapeDtypeStruct((2, fs, d), BF16),
+            pltpu.VMEM((toks, H * d), BF16),
+            pltpu.VMEM((H, 2, toks), F32),
+            pltpu.VMEM((2, 2, fs, d), BF16),
+            pltpu.VMEM((2, fs, d), BF16),
         ),
         in_specs=[anywhere] * 2 + [vmem] * 3 + [anywhere] * 2,
-        out_specs=(anywhere, vmem, vmem, vmem),
+        out_specs=(vmem,) * 4,
         scratch_shapes=[
             pltpu.VMEM((2, rows), jnp.int32),
             pltpu.VMEM((2, rows), F32),
-            pltpu.VMEM((toks, H * d), BF16),
             pltpu.VMEM((3, fc, d), F32),
             pltpu.VMEM((2 * rows, d), BF16),
             pltpu.VMEM((peers, 2, cap, d), BF16),
@@ -561,10 +546,10 @@
             dma((peers,)),
             dma((peers,)),
             dma((peers,)),
-            dma((2 * H + 3,)),
+            dma((2 * H + 2,)),
         ],
         compiler_params=pltpu.CompilerParams(
-            collective_id=0, has_side_effects=True, vmem_limit_bytes=67_000_000
+            collective_id=0, has_side_effects=True, vmem_limit_bytes=60_000_000
         ),
         name="moe_backward",
     )(
@@ -579,12 +564,11 @@
     gtok, gprob, gin, gout = pl.pallas_call(
         copy_kernel,
         out_shape=tuple(jax.ShapeDtypeStruct(a.shape, a.dtype) for a in (gtok, gprob, gin, gout)),
-        in_specs=[anywhere] * 4,
+        in_specs=[vmem] * 4,
         out_specs=(anywhere,) * 4,
-        scratch_shapes=[pltpu.VMEM(a.shape, a.dtype) for a in (gtok, gprob, gin, gout)]
-        + [dma((10,)), dma((10,))],
+        scratch_shapes=[dma((4,))],
         name="results",
-    )(gtok, gprob, gin, gout)
+    )(*(pltpu.with_memory_space_constraint(a, pltpu.VMEM) for a in (gtok, gprob, gin, gout)))
     return gtok, jnp.transpose(gprob, (2, 0, 1)), gin, gout
 
 

time: 130 us -> 128 us (0.985)
  Pallas kernels: 129 us -> 127 us
where the time goes in v4:
time: 128 us
  Pallas kernels  127 us (99%)
    pallas_call x1, Pallas kernels, body(): pl.pallas_call(functools.partial(kernel, (ng, toks, d, fs, cap)), out_sha...  125 us

profile of v4, /device:TPU:0, one launch (start us, length us, event | category | flops | bytes accessed | tf_op | source)
XLA Modules:
  0.0 127.6 jit_solution(204396963532761441)
XLA Ops:
  0.6 125.4 %moe_backward.1 = (bf16[128,4096]{1,0:T(8,128)(2,1)S(1)}, f32[8,2,128]{2,1,0:T(2,128)S(1)}, bf16[2,2,224,512]{3,2,1,0:T(8,128)(2,1)S(1)}, bf16[2,224,512]{2,1,0:T(8,128)(2,1)S(1)}) custom-call(bf16[128,4096]{1,0:T(8,128)(2,1)} %tok.1, bf16[128,4096]{1,0:T(8,128)(2,1)} %cot.1, s32[8,2,128]{2,1,0:T(2,128)} %bitcast.4, s32[8,2,128]{2,1,0:T(2,128)} %bitcast.5, ...), custom_call_target="tpu_custom_call" | custom-call | tf_op jit(solution)/shard_map/moe_backward/pallas_call | solution.py:512
  126.0 1.5 %results.1 = (bf16[128,4096]{1,0:T(8,128)(2,1)}, f32[8,2,128]{2,1,0:T(2,128)}, bf16[2,2,224,512]{3,2,1,0:T(8,128)(2,1)}, bf16[2,224,512]{2,1,0:T(8,128)(2,1)}) custom-call(bf16[128,4096]{1,0:T(8,128)(2,1)S(1)} %get-tuple-element.12.refs_0_, f32[8,2,128]{2,1,0:T(2,128)S(1)} %get-tuple-element.13.refs_1_, ...), custom_call_target="tpu_custom_call" | custom-call | tf_op jit(solution)/shard_map/results/pallas_call | solution.py:564

commit v5 on v4

--- a/solution.py
+++ b/solution.py
@@ -52,6 +52,9 @@
     gprob,
     gin,
     gout,
+    ids_buf,
+    slots_buf,
+    probs_buf,
     place_row,
     prob_row,
     far_acc,
@@ -153,11 +156,12 @@
     local = [pltpu.make_async_copy(a, b, l_sem.at[n]) for n, (a, b) in enumerate(local)]
     for c in local:
         c.start()
-    place = ids_in[...] * cap + slots_in[...]
-    probs = probs_in[...].astype(F32)
-    for k in range(2):
-        place_row[k : k + 1, :] = jnp.concatenate([place[n, k : k + 1] for n in range(H)], axis=1)
-        prob_row[k : k + 1, :] = jnp.concatenate([probs[n, k : k + 1] for n in range(H)], axis=1)
+    routes = ((ids_in, ids_buf), (slots_in, slots_buf), (probs_in, probs_buf))
+    routes = [
+        pltpu.make_async_copy(a, b, l_sem.at[2 * H + 2 + n]) for n, (a, b) in enumerate(routes)
+    ]
+    for c in routes:
+        c.start()
     pl.semaphore_wait(barrier, peers + 1)
 
     def wcopy(k, src, dst, to):
@@ -174,6 +178,13 @@
     for c in first:
         c.start()
 
+    for c in routes:
+        c.wait()
+    place = ids_buf[...] * cap + slots_buf[...]
+    probs = probs_buf[...].astype(F32)
+    for k in range(2):
+        place_row[k : k + 1, :] = jnp.concatenate([place[n, k : k + 1] for n in range(H)], axis=1)
+        prob_row[k : k + 1, :] = jnp.concatenate([probs[n, k : k + 1] for n in range(H)], axis=1)
     for c in local:
         c.wait()
 
@@ -289,12 +300,19 @@
     xs_wait(2)
     sweep(4, lambda n: (x + 2 + n) % NX, lambda n: n * 0 + 2)
 
-    before = slots - jb
+    share = min(2, per)
+    held = peers - per // share
+    before = held * cap
+    for i in range((BLOCKS - 1) * share, BLOCKS * share - 1):
+        xs_wait(i, share)
+        block(far, i, share)
     for m in range(3):
         far_acc[m] = dot_nn(
             acts[far, m, :, :, 0:before].reshape(fc, before),
-            xs_all[0 : peers - per, m // 2].reshape(before, d),
+            xs_all[0:held, m // 2].reshape(before, d),
         )
+    xs_wait(BLOCKS * share - 1, share)
+
     def give(i):
         for k in range(per):
             t = i * per + k
@@ -354,14 +372,11 @@
                 rs_far[side, p, m].astype(F32) + mine
             ).astype(BF16)
 
-    share = min(2, per)
-    for i in range((BLOCKS - 1) * share, BLOCKS * share):
-        xs_wait(i, share)
-        block(far, i, share)
+    block(far, BLOCKS * share - 1, share)
     for m in range(3):
         grad = far_acc[m] + dot_nn(
-            acts[far, m, :, :, before:slots].reshape(fc, jb),
-            xs_all[peers - per : peers, m // 2].reshape(jb, d),
+            acts[far, m, :, :, before:slots].reshape(fc, slots - before),
+            xs_all[held:peers, m // 2].reshape(slots - before, d),
         )
         acts[far, m, :, :, 0:d] = grad.astype(BF16).reshape(NH, fs, d)
     for p in (0, 1):
@@ -517,9 +532,12 @@
             pltpu.VMEM((2, 2, fs, d), BF16),
             pltpu.VMEM((2, fs, d), BF16),
         ),
-        in_specs=[anywhere] * 2 + [vmem] * 3 + [anywhere] * 2,
+        in_specs=[anywhere] * 7,
         out_specs=(vmem,) * 4,
         scratch_shapes=[
+            pltpu.VMEM((H, 2, toks), jnp.int32),
+            pltpu.VMEM((H, 2, toks), jnp.int32),
+            pltpu.VMEM((H, 2, toks), BF16),
             pltpu.VMEM((2, rows), jnp.int32),
             pltpu.VMEM((2, rows), F32),
             pltpu.VMEM((3, fc, d), F32),
@@ -546,7 +564,7 @@
             dma((peers,)),
             dma((peers,)),
             dma((peers,)),
-            dma((2 * H + 2,)),
+            dma((2 * H + 2 + 3,)),
         ],
         compiler_params=pltpu.CompilerParams(
             collective_id=0, has_side_effects=True, vmem_limit_bytes=60_000_000

time: 128 us -> 128 us (level)
  no operation moved by 1% of the time
where the time goes in v5:
time: 128 us; the launch traced here: 127 us
  Pallas kernels  127 us (99%)
    pallas_call x1, Pallas kernels, body(): pl.pallas_call(functools.partial(kernel, (ng, toks, d, fs, cap)), out_sha...  125 us

profile of v5, /device:TPU:0, one launch (start us, length us, event | category | flops | bytes accessed | tf_op | source)
XLA Modules:
  0.0 127.5 jit_solution(3448034144858594177)
XLA Ops:
  0.6 125.2 %moe_backward.1 = (bf16[128,4096]{1,0:T(8,128)(2,1)S(1)}, f32[8,2,128]{2,1,0:T(2,128)S(1)}, bf16[2,2,224,512]{3,2,1,0:T(8,128)(2,1)S(1)}, bf16[2,224,512]{2,1,0:T(8,128)(2,1)S(1)}) custom-call(bf16[128,4096]{1,0:T(8,128)(2,1)} %tok.1, bf16[128,4096]{1,0:T(8,128)(2,1)} %cot.1, s32[8,2,128]{2,1,0:T(2,128)} %bitcast.4, s32[8,2,128]{2,1,0:T(2,128)} %bitcast.5, ...), custom_call_target="tpu_custom_call" | custom-call | tf_op jit(solution)/shard_map/moe_backward/pallas_call | solution.py:527
  125.8 1.5 %results.1 = (bf16[128,4096]{1,0:T(8,128)(2,1)}, f32[8,2,128]{2,1,0:T(2,128)}, bf16[2,2,224,512]{3,2,1,0:T(8,128)(2,1)}, bf16[2,224,512]{2,1,0:T(8,128)(2,1)}) custom-call(bf16[128,4096]{1,0:T(8,128)(2,1)S(1)} %get-tuple-element.12.refs_0_, f32[8,2,128]{2,1,0:T(2,128)S(1)} %get-tuple-element.13.refs_1_, ...), custom_call_target="tpu_custom_call" | custom-call | tf_op jit(solution)/shard_map/results/pallas_call | solution.py:582

commit v6 on v5

--- a/solution.py
+++ b/solution.py
@@ -250,7 +250,7 @@
         gate = dot_nt(wg, xb)
         up = dot_nt(wu, xb)
         dh = dot_nt(wo, sb)
-        sg = 0.5 * jnp.tanh(0.5 * gate) + 0.5
+        sg = 1.0 / (1.0 + jnp.exp(-gate))
         a = gate * sg
         du = dh * a
         dg = dh * up * (sg + a * (1.0 - sg))

time: 128 us -> 128 us (level)
  no operation moved by 1% of the time
where the time goes in v6:
time: 128 us
  Pallas kernels  127 us (99%)
    pallas_call x1, Pallas kernels, body(): pl.pallas_call(functools.partial(kernel, (ng, toks, d, fs, cap)), out_sha...  125 us

profile of v6, /device:TPU:0, one launch (start us, length us, event | category | flops | bytes accessed | tf_op | source)
XLA Modules:
  0.0 127.6 jit_solution(17532872464275811546)
XLA Ops:
  0.6 125.3 %moe_backward.1 = (bf16[128,4096]{1,0:T(8,128)(2,1)S(1)}, f32[8,2,128]{2,1,0:T(2,128)S(1)}, bf16[2,2,224,512]{3,2,1,0:T(8,128)(2,1)S(1)}, bf16[2,224,512]{2,1,0:T(8,128)(2,1)S(1)}) custom-call(bf16[128,4096]{1,0:T(8,128)(2,1)} %tok.1, bf16[128,4096]{1,0:T(8,128)(2,1)} %cot.1, s32[8,2,128]{2,1,0:T(2,128)} %bitcast.4, s32[8,2,128]{2,1,0:T(2,128)} %bitcast.5, ...), custom_call_target="tpu_custom_call" | custom-call | tf_op jit(solution)/shard_map/moe_backward/pallas_call | solution.py:527
  126.0 1.5 %results.1 = (bf16[128,4096]{1,0:T(8,128)(2,1)}, f32[8,2,128]{2,1,0:T(2,128)}, bf16[2,2,224,512]{3,2,1,0:T(8,128)(2,1)}, bf16[2,224,512]{2,1,0:T(8,128)(2,1)}) custom-call(bf16[128,4096]{1,0:T(8,128)(2,1)S(1)} %get-tuple-element.12.refs_0_, f32[8,2,128]{2,1,0:T(2,128)S(1)} %get-tuple-element.13.refs_1_, ...), custom_call_target="tpu_custom_call" | custom-call | tf_op jit(solution)/shard_map/results/pallas_call | solution.py:582
